TPU v7x, 32 devices: a 4x4x1 block of a 4x4x8 slice. The times are simulated.
32 devices in a mesh: batch: 1 (over z), cols: 4 (over y), rows: 8 (over x, core).
Axes of the slice: x: 4, y: 4, z: 1, core: 2. Of those that a mesh axis runs over, the one named last changes fastest.
The devices are a block of a 4x4x8 slice.
Arguments:
- frames: bfloat16 [16, 1, 256, 384, 8], P(None, 'batch', 'rows', 'cols')
- h_init: float32 [1, 256, 384, 64], P('batch', 'rows', 'cols')
- w_x: bfloat16 [3, 3, 8, 192], replicated
- w_hzr: bfloat16 [3, 3, 64, 128], replicated
- w_hn: bfloat16 [3, 3, 64, 64], replicated
- gate_bias: float32 [192], replicated
Outputs:
- output 1: bfloat16 [16, 1, 256, 384, 64], P(None, 'batch', 'rows', 'cols')
- output 2: float32 [1, 256, 384, 64], P('batch', 'rows', 'cols')
All inputs are finite; a program needn't handle non-finite values.
Results may differ from a plain program's by a relative error of at most 0.00386505.
Values are sent between devices in bfloat16 or wider.
A program may use at most 768 MiB of HBM per device.

v0:
```python
import jax
import jax.numpy as jnp
from jax import lax
from jax.sharding import PartitionSpec as P, NamedSharding


def with_halo(tile, width, n_rows, n_cols):
    tile_h = tile.shape[-3]
    tile_w = tile.shape[-2]
    down_pairs = [(dev_idx, dev_idx + 1) for dev_idx in range(n_rows - 1)]
    up_pairs = [(dev_idx + 1, dev_idx) for dev_idx in range(n_rows - 1)]
    from_above = lax.ppermute(tile[..., tile_h - width:, :, :], 'rows', down_pairs)
    from_below = lax.ppermute(tile[..., :width, :, :], 'rows', up_pairs)
    tall_tile = jnp.concatenate([from_above, tile, from_below], axis=-3)
    right_pairs = [(dev_idx, dev_idx + 1) for dev_idx in range(n_cols - 1)]
    left_pairs = [(dev_idx + 1, dev_idx) for dev_idx in range(n_cols - 1)]
    from_left = lax.ppermute(tall_tile[..., tile_w - width:, :], 'cols', right_pairs)
    from_right = lax.ppermute(tall_tile[..., :width, :], 'cols', left_pairs)
    return jnp.concatenate([from_left, tall_tile, from_right], axis=-2)


def im2col_conv(padded, w_mat):
    out_h = padded.shape[-3] - 2
    out_w = padded.shape[-2] - 2
    tap_list = [padded[..., row_off:row_off + out_h, col_off:col_off + out_w, :] for row_off in range(3) for col_off in range(3)]
    patches = jnp.concatenate(tap_list, axis=-1)
    return jnp.einsum('...k,kg->...g', patches, w_mat, preferred_element_type=jnp.float32)


def solution(mesh):
    n_rows = mesh.shape['rows']
    n_cols = mesh.shape['cols']
    frame_spec = P(None, 'batch', 'rows', 'cols', None)
    state_spec = P('batch', 'rows', 'cols', None)

    def local_fn(frames, h_init, w_x, w_hzr, w_hn, gate_bias):
        n_hidden = h_init.shape[-1]
        wx_mat = w_x.reshape(-1, w_x.shape[-1])
        whzr_mat = w_hzr.reshape(-1, w_hzr.shape[-1])
        whn_mat = w_hn.reshape(-1, w_hn.shape[-1])
        frames_pad = with_halo(frames, 1, n_rows, n_cols)

        def one_step(h_prev, frame_pad):
            gate_x = im2col_conv(frame_pad, wx_mat) + gate_bias
            h_pad = with_halo(h_prev.astype(jnp.bfloat16), 1, n_rows, n_cols)
            zr_gates = jax.nn.sigmoid(gate_x[..., :2 * n_hidden] + im2col_conv(h_pad, whzr_mat))
            update = zr_gates[..., :n_hidden]
            reset_pad = with_halo((zr_gates[..., n_hidden:] * h_prev).astype(jnp.bfloat16), 1, n_rows, n_cols)
            candidate = jnp.tanh(gate_x[..., 2 * n_hidden:] + im2col_conv(reset_pad, whn_mat))
            h_next = (1.0 - update) * candidate + update * h_prev
            return h_next, h_next.astype(jnp.bfloat16)

        h_last, h_seq = lax.scan(one_step, h_init, frames_pad)
        return h_seq, h_last

    return jax.shard_map(local_fn, mesh=mesh, in_specs=(frame_spec, state_spec, P(), P(), P(), P()), out_specs=(frame_spec, state_spec), check_vma=False)
```

profile of v0, /device:TPU:97, one launch (start us, length us, event | category | flops | bytes accessed | tf_op | source)
XLA Modules:
  0.0 1111.0 jit_solution(935093001700741279)
XLA Ops:
  30.4 1079.2 %while.12 = (s32[]{:T(128)}, f32[1,32,96,64]{3,2,1,0:T(8,128)S(1)}, bf16[16,1,32,96,64]{3,4,2,1,0:T(8,128)(2,1)}, bf16[16,1,34,98,8]{3,4,2,1,0:T(8,128)(2,1)}, b...) while((s32[]{:T(128)}, f32[1,32,96,64]{3,2,1,0:T(8,128)S(1)}, ...), condition=%wide.region_1.2_spmd, body=%wide.region_0.1_spmd.sunk | while | flops 775937024 | bytes 59772232 | solution.py:53
  41.6 5.1 collective-permute-start.3
  50.7 9.1 concatenate.59
  81.9 9.3 concatenate.60
  91.2 4.8 fusion.55
  99.4 4.8 collective-permute-start.1
  118.1 9.1 concatenate.59
  149.4 9.3 concatenate.60
  158.7 4.8 fusion.55
  166.9 4.8 collective-permute-start.1
  185.6 9.1 concatenate.59
  216.9 9.3 concatenate.60
  226.2 4.8 fusion.55
  234.4 4.8 collective-permute-start.1
  253.1 9.1 concatenate.59
  284.4 9.3 concatenate.60
  293.7 4.8 fusion.55
  301.9 4.8 collective-permute-start.1
  320.6 9.1 concatenate.59
  351.8 9.3 concatenate.60
  361.1 4.8 fusion.55
  369.4 4.8 collective-permute-start.1
  388.0 9.1 concatenate.59
  419.3 9.3 concatenate.60
  428.6 4.8 fusion.55
  436.8 4.8 collective-permute-start.1
  455.5 9.1 concatenate.59
  486.8 9.3 concatenate.60
  496.1 4.8 fusion.55
  504.3 4.8 collective-permute-start.1
  523.0 9.1 concatenate.59
  554.3 9.3 concatenate.60
  563.6 4.8 fusion.55
  571.8 4.8 collective-permute-start.1
  590.5 9.1 concatenate.59
  621.7 9.3 concatenate.60
  631.1 4.8 fusion.55
  639.3 4.8 collective-permute-start.1
  657.9 9.1 concatenate.59
  689.2 9.3 concatenate.60
  698.5 4.8 fusion.55
  706.7 4.8 collective-permute-start.1
  725.4 9.1 concatenate.59
  756.7 9.3 concatenate.60
  766.0 4.8 fusion.55
  774.2 4.8 collective-permute-start.1
  792.9 9.1 concatenate.59
  824.2 9.3 concatenate.60
  833.5 4.8 fusion.55
  841.7 4.8 collective-permute-start.1
  860.4 9.1 concatenate.59
  891.7 9.3 concatenate.60
  901.0 4.8 fusion.55
  909.2 4.8 collective-permute-start.1
  927.8 9.1 concatenate.59
  959.1 9.3 concatenate.60
  968.4 4.8 fusion.55
  976.7 4.8 collective-permute-start.1
  995.3 9.1 concatenate.59
  1026.6 9.3 concatenate.60
  1035.9 4.8 fusion.55
  1062.8 9.1 concatenate.59
  1094.1 9.3 concatenate.60
  1103.4 4.8 fusion.55
  (751 shorter events, 662.0 us)
Async XLA Ops:
  14.8 8.0 collective-permute-start.10
  30.7 9.6 collective-permute-start
  32.6 7.6 collective-permute-start.1
  40.3 7.8 collective-permute-start.2
  97.5 10.7 collective-permute-start
  99.4 8.8 collective-permute-start.1
  108.3 7.3 collective-permute-start.2
  139.0 6.8 collective-permute-start.6
  165.0 10.7 collective-permute-start
  166.9 8.8 collective-permute-start.1
  175.7 7.3 collective-permute-start.2
  206.4 6.8 collective-permute-start.6
  232.4 10.7 collective-permute-start
  234.4 8.8 collective-permute-start.1
  243.2 7.3 collective-permute-start.2
  273.9 6.8 collective-permute-start.6
  299.9 10.7 collective-permute-start
  301.9 8.7 collective-permute-start.1
  310.7 7.3 collective-permute-start.2
  341.4 6.8 collective-permute-start.6
  367.4 10.7 collective-permute-start
  369.4 8.7 collective-permute-start.1
  378.1 7.3 collective-permute-start.2
  408.9 6.8 collective-permute-start.6
  434.9 10.7 collective-permute-start
  436.8 8.7 collective-permute-start.1
  445.6 7.3 collective-permute-start.2
  476.3 6.8 collective-permute-start.6
  502.4 10.7 collective-permute-start
  504.3 8.7 collective-permute-start.1
  513.1 7.3 collective-permute-start.2
  543.8 6.8 collective-permute-start.6
  569.8 10.7 collective-permute-start
  571.8 8.7 collective-permute-start.1
  580.6 7.3 collective-permute-start.2
  611.3 6.8 collective-permute-start.6
  637.3 10.7 collective-permute-start
  639.3 8.7 collective-permute-start.1
  648.0 7.3 collective-permute-start.2
  678.8 6.8 collective-permute-start.6
  704.8 10.7 collective-permute-start
  706.7 8.7 collective-permute-start.1
  715.5 7.3 collective-permute-start.2
  746.2 6.8 collective-permute-start.6
  772.3 10.7 collective-permute-start
  774.2 8.7 collective-permute-start.1
  783.0 7.3 collective-permute-start.2
  813.7 6.8 collective-permute-start.6
  839.7 10.7 collective-permute-start
  841.7 8.7 collective-permute-start.1
  850.5 7.3 collective-permute-start.2
  881.2 6.8 collective-permute-start.6
  907.2 10.7 collective-permute-start
  909.2 8.7 collective-permute-start.1
  917.9 7.3 collective-permute-start.2
  948.7 6.8 collective-permute-start.6
  974.7 10.7 collective-permute-start
  976.7 8.7 collective-permute-start.1
  985.4 7.3 collective-permute-start.2
  1016.1 6.8 collective-permute-start.6
  1042.2 10.7 collective-permute-start
  1044.1 8.7 collective-permute-start.1
  1052.9 7.3 collective-permute-start.2
  1083.6 6.8 collective-permute-start.6
  (88 other events, 405.8 us)
where the time goes:
time: 1130 us; the launch traced here: 1110 us
  local copies, waits for them, and re-layouts  451 us (40%)
  starting transfers between devices  391 us (35%)
  matrix products  177 us (16%)
  other arithmetic  72.1 us (6%)
  waiting for transfers between devices  16.8 us (1%)
    concatenate x48, local copies, waits for them, and re-layouts, im2col_conv(): patches = jnp.concatenate(tap_list, axis=-1)  297 us
    dot_general x48, matrix products, im2col_conv(): jnp.einsum('...k,kg->...g', patches, w_mat, preferred_element_type=jnp.fl...  177 us
    ppermute x33, starting transfers between devices, with_halo(): lax.ppermute(tall_tile[..., tile_w - width:, :], 'cols', right_pairs)  144 us
    ppermute x33, starting transfers between devices, with_halo(): lax.ppermute(tile[..., tile_h - width:, :, :], 'rows', down_pairs)  139 us
    slice x48, local copies, waits for them, and re-layouts, im2col_conv(): padded[..., row_off:row_off + out_h, col_off:col_off + out_w, :]  86.4 us
    ppermute x33, starting transfers between devices, with_halo(): from_below = lax.ppermute(tile[..., :width, :, :], 'rows', up_pairs)  64.2 us
    concatenate x64, other arithmetic, with_halo(): tall_tile = jnp.concatenate([from_above, tile, from_below], axis=-3)  44.8 us
    ppermute x33, starting transfers between devices, with_halo(): from_right = lax.ppermute(tall_tile[..., :width, :], 'cols', left_pairs)  43.3 us
  transfers between devices with their start and end apart: 132, of which 17 were waited for; matrix products, arithmetic and copies ran while one was open for 10% of the time, Pallas kernels for 0%

commit v1 on v0

v1 whole, which is shorter than its diff:
```python
import functools

import jax
import jax.numpy as jnp
from jax import lax
from jax.experimental import pallas as pl
from jax.experimental.pallas import tpu as pltpu
from jax.sharding import PartitionSpec as P

FUSE = 2
CHUNK = 4
MARGIN = 16
COMP = 112
DIRS = ((-1, 0), (1, 0), (0, -1), (0, 1), (-1, -1), (-1, 1), (1, -1), (1, 1))


def frames_with_halo(frames, width, n_rows, n_cols):
    down = [(i, i + 1) for i in range(n_rows - 1)]
    up = [(i + 1, i) for i in range(n_rows - 1)]
    above = lax.ppermute(frames[:, -width:], 'rows', down)
    below = lax.ppermute(frames[:, :width], 'rows', up)
    tall = jnp.concatenate([above, frames, below], axis=1)
    right = [(i, i + 1) for i in range(n_cols - 1)]
    left = [(i + 1, i) for i in range(n_cols - 1)]
    from_left = lax.ppermute(tall[..., -width:], 'cols', right)
    from_right = lax.ppermute(tall[..., :width], 'cols', left)
    return jnp.concatenate([from_left, tall, from_right], axis=-1)


def fold_rows(w, order):
    n_gates = w.shape[-1] // 64
    blocks = []
    for rho in order:
        outs = []
        for o in range(2):
            a = rho - o + 1
            outs.append(w[a] if 0 <= a <= 2 else jnp.zeros_like(w[0]))
        both = jnp.stack([b.reshape(3, w.shape[2], n_gates, 64) for b in outs], axis=3)
        blocks.append(both.reshape(3, w.shape[2], n_gates * 128))
    return jnp.stack(blocks, axis=1)


def kernel(dims, x_ref, h_ref, wzr_ref, wn_ref, b_ref, seq_ref, last_ref,
           hs, rh, zs, xl, stage, row_in, col_in, cor_in, send_sem, recv_sem, out_sem):
    n_steps, n_pairs, width, n_rows, n_cols = dims
    k = FUSE
    first = k + 1
    my_row = lax.axis_index('rows')
    my_col = lax.axis_index('cols')

    def there(di, dj):
        r, c = my_row + di, my_col + dj
        return jnp.logical_and(jnp.logical_and(r >= 0, r < n_rows), jnp.logical_and(c >= 0, c < n_cols))

    barrier = pltpu.get_barrier_semaphore()
    for di, dj in DIRS:
        @pl.when(there(di, dj))
        def _():
            pl.semaphore_signal(barrier, inc=1, device_id={'rows': my_row + di, 'cols': my_col + dj},
                                device_id_type=pl.DeviceIdType.MESH)

    hs[...] = jnp.zeros_like(hs)
    rh[...] = jnp.zeros_like(rh)
    for q in range(n_pairs):
        hs[first + q, MARGIN:MARGIN + width, :] = h_ref[q].T

    n_peers = sum(there(di, dj).astype(jnp.int32) for di, dj in DIRS)
    pl.semaphore_wait(barrier, n_peers)

    def src_of(di, dj):
        rows = {-1: pl.ds(first, k), 1: pl.ds(first + n_pairs - k, k), 0: pl.ds(first, n_pairs)}[di]
        cols = {-1: pl.ds(MARGIN, 8), 1: pl.ds(MARGIN + width - 8, 8), 0: pl.ds(MARGIN, width)}[dj]
        return rows, cols

    def dst_of(di, dj):
        rows = {-1: pl.ds(first + n_pairs, k), 1: pl.ds(first - k, k), 0: pl.ds(first, n_pairs)}[di]
        cols = {-1: pl.ds(MARGIN + width, 8), 1: pl.ds(MARGIN - 8, 8), 0: pl.ds(MARGIN, width)}[dj]
        return rows, cols

    def landing(d, par):
        if d < 2:
            return row_in.at[par, d]
        if d < 4:
            return col_in.at[par, d - 2]
        return cor_in.at[par, d - 4]

    def copy_of(d, par):
        di, dj = DIRS[d]
        rows, cols = src_of(di, dj)
        return pltpu.make_async_remote_copy(
            src_ref=hs.at[rows, cols, :], dst_ref=landing(d, par), send_sem=send_sem.at[d],
            recv_sem=recv_sem.at[par, d], device_id={'rows': my_row + di, 'cols': my_col + dj},
            device_id_type=pl.DeviceIdType.MESH)

    lane = lax.broadcasted_iota(jnp.int32, (1, 1, 128), 2)
    low = lane < 64

    def conv(src, s, q0, n, w_ref):
        parts = []
        for c in range(3):
            cols = pl.ds(MARGIN - 9 + c, COMP)
            own = src[q0:q0 + n, cols, :]
            edge = jnp.where(low, src[q0 + 1:q0 + 1 + n, cols, :], src[q0 - 1:q0 - 1 + n, cols, :])
            parts += [own.astype(jnp.bfloat16), edge.astype(jnp.bfloat16)]
        parts.append(xl[s, q0 - 1:q0 - 1 + n])
        lhs = jnp.concatenate(parts, axis=-1).reshape(n * COMP, 7 * 128)
        return jnp.dot(lhs, w_ref[...], preferred_element_type=jnp.float32)

    def sigmoid(v):
        return 0.5 * jnp.tanh(0.5 * v) + 0.5

    def zr_chunk(s, q0, n):
        acc = conv(hs, s, q0, n, wzr_ref)
        z = sigmoid(acc[:, :128] + b_ref[0:1, :])
        r = sigmoid(acc[:, 128:] + b_ref[1:2, :])
        zs[q0:q0 + n] = z.reshape(n, COMP, 128)
        rh[q0:q0 + n, MARGIN - 8:MARGIN - 8 + COMP, :] = r.reshape(n, COMP, 128) * hs[q0:q0 + n, MARGIN - 8:MARGIN - 8 + COMP, :]

    def n_chunk(s, q0, n, slot, last):
        acc = conv(rh, s, q0, n, wn_ref)
        cand = jnp.tanh(acc + b_ref[2:3, :]).reshape(n, COMP, 128)
        h = hs[q0:q0 + n, MARGIN - 8:MARGIN - 8 + COMP, :]
        h_new = cand + zs[q0:q0 + n] * (h - cand)
        inner = h_new[:, 8:8 + width, :]
        if last:
            hs[q0:q0 + n, MARGIN:MARGIN + width, :] = inner
        else:
            hs[q0:q0 + n, MARGIN - 8:MARGIN - 8 + COMP, :] = h_new
        for i in range(n):
            q = q0 + i - first
            if 0 <= q < n_pairs:
                stage[slot, q] = inner[i].T.astype(jnp.bfloat16)

    def chunks(lo, hi):
        for q0 in range(lo, hi, CHUNK):
            yield q0, min(CHUNK, hi - q0)

    def build_x(t, s):
        x = x_ref[t].astype(jnp.float32)
        taps = (pltpu.roll(x, 1, 1).astype(jnp.bfloat16), x_ref[t], pltpu.roll(x, 127, 1).astype(jnp.bfloat16))
        zero = jnp.zeros((32, 128), jnp.bfloat16)
        for i in range(n_pairs + 2 * k):
            both = jnp.concatenate([tap[16 * i:16 * i + 32] for tap in taps] + [zero], axis=0)
            xl[s, i] = both.T[:COMP]

    def out_copy(t, slot):
        return pltpu.make_async_copy(stage.at[slot], seq_ref.at[t], out_sem.at[slot])

    def period(p, carry):
        par = lax.rem(p, 2)
        for d, (di, dj) in enumerate(DIRS):
            @pl.when(there(di, dj))
            def _():
                copy_of(d, par).start()
        for s in range(k):
            build_x(p * k + s, s)
        for d, (di, dj) in enumerate(DIRS):
            @pl.when(there(-di, -dj))
            def _():
                copy_of(d, par).wait_recv()
                rows, cols = dst_of(di, dj)
                hs[rows, cols, :] = landing(d, par)[...]
        for s in range(k):
            ext = k - 1 - s
            t = p * k + s
            slot = s % 2 if k % 2 == 0 else lax.rem(t, 2)
            for q0, n in chunks(first - ext - 1, first + n_pairs + ext + 1):
                zr_chunk(s, q0, n)
            if s == 0:
                for d, (di, dj) in enumerate(DIRS):
                    @pl.when(there(di, dj))
                    def _():
                        copy_of(d, par).wait_send()

            @pl.when(t >= 2)
            def _():
                out_copy(t - 2, slot).wait()
            for q0, n in chunks(first - ext, first + n_pairs + ext):
                n_chunk(s, q0, n, slot, s == k - 1)
            out_copy(t, slot).start()
            if s < k - 1:
                @pl.when(my_row == 0)
                def _():
                    hs[first - ext:first, :, :] = jnp.zeros((ext, 128, 128), jnp.float32)

                @pl.when(my_row == n_rows - 1)
                def _():
                    hs[first + n_pairs:first + n_pairs + ext, :, :] = jnp.zeros((ext, 128, 128), jnp.float32)

                @pl.when(my_col == 0)
                def _():
                    hs[:, MARGIN - 8:MARGIN, :] = jnp.zeros((hs.shape[0], 8, 128), jnp.float32)

                @pl.when(my_col == n_cols - 1)
                def _():
                    hs[:, MARGIN + width:MARGIN + width + 8, :] = jnp.zeros((hs.shape[0], 8, 128), jnp.float32)
        return carry

    lax.fori_loop(0, n_steps // k, period, 0)
    for q in range(n_pairs):
        last_ref[q] = hs[first + q, MARGIN:MARGIN + width, :].T
    for t in range(n_steps - 2, n_steps):
        out_copy(t, t % 2).wait()


def solution(mesh):
    n_rows = mesh.shape['rows']
    n_cols = mesh.shape['cols']
    frame_spec = P(None, 'batch', 'rows', 'cols', None)
    state_spec = P('batch', 'rows', 'cols', None)

    def local_fn(frames, h_init, w_x, w_hzr, w_hn, gate_bias):
        n_steps, _, tile_h, width, c_in = frames.shape
        n_hidden = h_init.shape[-1]
        k = FUSE
        n_pairs = tile_h // 2
        halo = 2 * k
        x = frames_with_halo(frames[:, 0].transpose(0, 1, 3, 2), halo, n_rows, n_cols)
        x = jnp.pad(x, ((0, 0), (1, 1), (0, 0), (8 - halo, 128 - 8 - width - halo)))
        x = x.reshape(n_steps, (tile_h + 2 * halo + 2) * c_in, 128)
        h0 = h_init[0].transpose(0, 2, 1).reshape(n_pairs, 2 * n_hidden, width)
        wx = fold_rows(w_x, (-1, 0, 1, 2)).reshape(96, 384)
        wx = jnp.pad(wx, ((0, 32), (0, 0)))
        wzr = jnp.concatenate([fold_rows(w_hzr, (0, 1, 2, -1)).reshape(768, 256), wx[:, :256]], axis=0)
        wn = jnp.concatenate([fold_rows(w_hn, (0, 1, 2, -1)).reshape(768, 128), wx[:, 256:]], axis=0)
        bias = jnp.tile(gate_bias.reshape(3, 1, n_hidden), (1, 2, 1)).reshape(3, 128)
        n_buf = n_pairs + 2 * k + 2
        vmem = pl.BlockSpec(memory_space=pltpu.VMEM)
        seq, last = pl.pallas_call(
            functools.partial(kernel, (n_steps, n_pairs, width, n_rows, n_cols)),
            out_shape=(jax.ShapeDtypeStruct((n_steps, n_pairs, 128, width), jnp.bfloat16),
                       jax.ShapeDtypeStruct((n_pairs, 128, width), jnp.float32)),
            in_specs=[vmem] * 5,
            out_specs=(pl.BlockSpec(memory_space=pl.ANY), vmem),
            scratch_shapes=[
                pltpu.VMEM((n_buf, 128, 128), jnp.float32),
                pltpu.VMEM((n_buf, 128, 128), jnp.float32),
                pltpu.VMEM((n_buf, COMP, 128), jnp.float32),
                pltpu.VMEM((k, n_pairs + 2 * k, COMP, 128), jnp.bfloat16),
                pltpu.VMEM((2, n_pairs, 128, width), jnp.bfloat16),
                pltpu.VMEM((2, 2, k, width, 128), jnp.float32),
                pltpu.VMEM((2, 2, n_pairs, 8, 128), jnp.float32),
                pltpu.VMEM((2, 4, k, 8, 128), jnp.float32),
                pltpu.SemaphoreType.DMA((8,)),
                pltpu.SemaphoreType.DMA((2, 8)),
                pltpu.SemaphoreType.DMA((2,)),
            ],
            compiler_params=pltpu.CompilerParams(collective_id=0, has_side_effects=True),
        )(x, h0, wzr, wn, bias)
        seq = seq.reshape(n_steps, 1, tile_h, n_hidden, width).transpose(0, 1, 2, 4, 3)
        last = last.reshape(1, tile_h, n_hidden, width).transpose(0, 1, 3, 2)
        return seq, last

    return jax.shard_map(local_fn, mesh=mesh, in_specs=(frame_spec, state_spec, P(), P(), P(), P()), out_specs=(frame_spec, state_spec), check_vma=False)
```

time: 1130 us -> 132 us (0.12); the launches traced: 1110 us -> 132 us
  local copies, waits for them, and re-layouts: 451 us -> 25.5 us
  starting transfers between devices: 391 us -> 12.3 us
  matrix products: 177 us -> 0 us
  Pallas kernels: 0 us -> 86.2 us
  other arithmetic: 72.1 us -> 6.57 us
  waiting for transfers between devices: 16.8 us -> 0.51 us
    ppermute x132 -> x4, starting transfers between devices: 391 us -> 12.3 us  [the longest x1 4.6 us: frames_with_halo(): above = lax.ppermute(frames[:, -width:], 'rows', down)]
    concatenate x49 -> x0, local copies, waits for them, and re-layouts: 297 us -> none  [the longest x48 297 us: im2col_conv(): patches = jnp.concatenate(tap_list, axis=-1)]
    dot_general x48 -> x0, matrix products: 177 us -> none  [im2col_conv(): jnp.einsum('...k,kg->...g', patches, w_mat, preferred_element_type=jnp.fl...]
    pallas_call x0 -> x1, Pallas kernels: none -> 86.2 us  [local_fn(): pl.pallas_call(functools.partial(kernel, (n_steps, n_pairs, width, n_rows...]
    slice x82 -> x6, local copies, waits for them, and re-layouts: 88.7 us -> 3.41 us  [the longest x1 1.61 us: frames_with_halo(): from_left = lax.ppermute(tall[..., -width:], 'cols', right)]
    concatenate x97 -> x3, other arithmetic: 61.1 us -> 1.82 us  [the longest x1 0.8 us: local_fn(): jnp.concatenate([fold_rows(w_hzr, (0, 1, 2, -1)).reshape(768, 256), wx[:,...]
    while x162 -> x0, local copies, waits for them, and re-layouts: 22.6 us -> none
    dynamic_update_slice x32 -> x0, local copies, waits for them, and re-layouts: 18.6 us -> none  [local_fn(): h_last, h_seq = lax.scan(one_step, h_init, frames_pad)]
  transfers between devices with their start and end apart: 132 -> 4, of which waited for: 17 -> 1; matrix products, arithmetic and copies ran while one was open for 10% -> 7% of each run, Pallas kernels for 0% -> 0%
where the time goes in v1:
time: 132 us
  Pallas kernels  86.2 us (65%)
  local copies, waits for them, and re-layouts  25.5 us (19%)
  starting transfers between devices  12.3 us (9%)
  other arithmetic  6.57 us (5%)
    pallas_call x1, Pallas kernels, local_fn(): pl.pallas_call(functools.partial(kernel, (n_steps, n_pairs, width, n_rows...  86.2 us
    unnamed x20, local copies, waits for them, and re-layouts  14.6 us
    ppermute x1, starting transfers between devices, frames_with_halo(): above = lax.ppermute(frames[:, -width:], 'rows', down)  4.6 us
    ppermute x1, starting transfers between devices, frames_with_halo(): from_left = lax.ppermute(tall[..., -width:], 'cols', right)  4.42 us
    reshape x1, other arithmetic, local_fn(): x = x.reshape(n_steps, (tile_h + 2 * halo + 2) * c_in, 128)  4.01 us
  transfers between devices with their start and end apart: 4, of which 1 were waited for; matrix products, arithmetic and copies ran while one was open for 7% of the time, Pallas kernels for 0%

profile of v1, /device:TPU:97, one launch (start us, length us, event | category | flops | bytes accessed | tf_op | source)
XLA Modules:
  0.0 132.0 jit_solution(14406671771359139517)
XLA Ops:
  0.6 0.0 copy-start.2
  0.6 0.0 copy-start.3
  0.6 1.0 fusion.13
  1.7 4.6 %collective-permute-start = (bf16[16,4,8,96]{3,2,1,0:T(8,128)(2,1)S(1)}, bf16[16,4,8,96]{3,2,1,0:T(8,128)(2,1)S(1)}, u32[]{:S(2)}, u32[]{:S(2)}) collective-permute-start(bf16[16,4,8,96]{3,2,1,0:T(8,128)(2,1)S(1)} %get-tuple-element.8), channel_id=1, source_target_pairs={{0,1},{1,2},{2,3},{3,4},{4,5},{5,6},{6,7},{8,9},{9,10},{10,11},{11... | collective-permute-start | bytes 294920 | tf_op jit(solution)/shard_map/ppermute | solution.py:20
  6.3 2.0 %collective-permute-start.1 = (bf16[16,4,8,96]{3,2,1,0:T(8,128)(2,1)S(1)}, bf16[16,4,8,96]{3,2,1,0:T(8,128)(2,1)S(1)}, u32[]{:S(2)}, u32[]{:S(2)}) collective-permute-start(bf16[16,4,8,96]{3,2,1,0:T(8,128)(2,1)S(1)} %get-tuple-element.9), channel_id=1, source_target_pairs={{1,0},{2,1},{3,2},{4,3},{5,4},{6,5},{7,6},{9,8},{10,9},{11,10},{12... | collective-permute-start | bytes 294920 | tf_op jit(solution)/shard_map/ppermute | solution.py:21
  8.3 0.7 fusion.15
  9.0 0.1 stack_reshape_squeeze.39
  9.1 0.1 stack_reshape_squeeze.41
  9.2 0.1 stack_reshape_squeeze.40
  9.3 0.1 stack.53.clone
  9.4 0.1 stack_reshape.43
  9.6 0.1 stack_reshape.40
  9.7 0.1 pad_maximum_fusion.10
  9.8 0.1 stack_reshape.41
  9.9 0.1 stack_reshape.42
  10.1 0.0 copy-done.2
  10.1 0.1 stack_reshape_squeeze.36
  10.2 0.1 stack_reshape_squeeze.38
  10.3 0.1 stack_reshape_squeeze.37
  10.4 0.0 copy-done.3
  10.4 0.1 copy.84
  10.5 0.2 stack.57.clone
  10.7 0.1 stack_reshape.46
  10.8 0.1 copy.85
  10.9 0.1 stack.58.clone
  11.0 0.1 stack_reshape.47
  11.1 0.1 copy.72
  11.2 0.1 stack_reshape.44
  11.4 0.1 copy.73
  11.5 0.1 stack_reshape.45
  11.6 0.2 copy.81
  11.8 0.2 stack.48.clone
  12.1 0.2 stack_reshape.39
  12.2 0.2 copy.80
  12.5 0.3 stack.47.clone
  12.8 0.2 stack_reshape.38
  13.0 0.5 pad_maximum_fusion.4
  13.5 0.3 copy.63
  13.8 0.0 copy-start
  13.8 0.2 stack_reshape.36
  14.0 0.3 copy.64
  14.3 0.2 stack_reshape.37
  14.5 0.1 pad_maximum_fusion.2
  14.6 0.8 pad_maximum_fusion.1.wzr_ref
  15.4 0.0 collective-permute-done
  15.4 0.0 collective-permute-done.1
  15.4 0.0 copy-done
  15.4 0.3 pad_maximum_fusion
  15.7 1.6 %fusion.12 = (bf16[16,40,8,4]{3,2,1,0:T(8,128)(2,1)}, bf16[16,40,8,4]{3,2,1,0:T(8,128)(2,1)S(1)}) fusion(bf16[16,40,8,96]{3,2,1,0:T(8,128)(2,1)S(1)} %pad_maximum_fusion), kind=kLoop, calls=%fused_computation.35 | loop fusion | bytes 163840 | tf_op jit(solution)/shard_map/slice | solution.py:25
  17.3 2.3 %copy.78 = bf16[16,40,8,4]{1,2,3,0:T(8,128)(2,1)S(1)} copy(bf16[16,40,8,4]{3,2,1,0:T(8,128)(2,1)} %get-tuple-element.6) | data formatting | bytes 81920
  19.6 1.0 copy.79
  20.6 1.3 collective-permute-start.3
  21.9 4.4 %collective-permute-start.2 = (bf16[16,40,8,4]{1,2,3,0:T(8,128)(2,1)S(1)}, bf16[16,40,8,4]{1,2,3,0:T(8,128)(2,1)S(1)}, u32[]{:S(2)}, u32[]{:S(2)}) collective-permute-start(bf16[16,40,8,4]{1,2,3,0:T(8,128)(2,1)S(1)} %copy.78), channel_id=1, source_target_pairs={{0,8},{8,16},{16,24},{1,9},{9,17},{17,25},{2,10},{10,18},{18,26},{... | collective-permute-start | bytes 122888 | tf_op jit(solution)/shard_map/ppermute | solution.py:25
  26.4 0.7 pad_maximum_fusion.3.wn_ref
  27.1 0.1 tile.9
  27.2 0.6 tile.11.b_ref
  27.8 0.5 collective-permute-done.2
  28.3 0.9 copy.61
  29.2 0.0 collective-permute-done.3
  29.2 2.0 %copy.62 = bf16[16,40,8,4]{3,2,1,0:T(8,128)(2,1)} copy(bf16[16,40,8,4]{1,2,3,0:T(8,128)(2,1)S(1)} %collective-permute-done.3) | data formatting | bytes 81920 | tf_op jit(solution)/shard_map/ppermute | solution.py:26
  31.2 4.0 %fusion.3.x_ref = bf16[16,336,128]{2,1,0:T(8,128)(2,1)} fusion(bf16[16,40,8,4]{3,2,1,0:T(8,128)(2,1)} %copy.62, bf16[16,40,8,4]{3,2,1,0:T(8,128)(2,1)S(1)} %copy.61, bf16[16,4,8,96]{3,2,1,0:T(8,128)(2,1)S(1)} %collective-permute-done.1, bf16[16,32,8,96]{3,2,1,0:T(8,128)(2,1)S(1)} %bitcast.52, bf16[16,4,8,96]{3,2,1,0:T(8,128)(2,1)S(1)} %collective-permute-done), kind=kLoop, calls=%fused_computation.8 | loop fusion | flops 18579456 | bytes 2441216 | tf_op jit(solution)/shard_map/reshape | solution.py:220
  35.2 86.2 %shard_map.77 = (bf16[16,16,128,96]{3,2,1,0:T(8,128)(2,1)}, f32[16,128,96]{2,1,0:T(8,128)}) custom-call(bf16[16,336,128]{2,1,0:T(8,128)(2,1)} %fusion.3.x_ref, f32[16,128,96]{2,1,0:T(8,128)} %bitcast.55, bf16[896,256]{1,0:T(8,128)(2,1)} %pad_maximum_fusion.1.wzr_ref, bf16[896,128]{1,0:T(8,128)(2,1)} %pad_maximum_fusion.3.wn_ref, f32[3,128]{1,0:T(4,128)} %tile.11.b_ref), custom_call_target="tpu_custom_call" | custom-call | tf_op jit(solution)/shard_map/pallas_call | solution.py:229
  121.4 9.7 %copy.88 = bf16[16,1,32,96,64]{3,4,2,1,0:T(8,128)(2,1)} copy(bf16[16,1,32,96,64]{3,4,2,1,0:T(8,128)(2,1)} %bitcast.49) | data formatting | bytes 12582912
  131.1 1.0 copy.89
  (19 shorter events, 0.3 us)
Async XLA Ops:
  0.6 9.4 %copy-start.2 = (bf16[3,3,64,128]{3,2,1,0:T(8,128)(2,1)S(1)}, bf16[3,3,64,128]{3,2,1,0:T(8,128)(2,1)}, u32[]{:S(2)}) copy-start(bf16[3,3,64,128]{3,2,1,0:T(8,128)(2,1)} %param.9) | copy-start | bytes 442372
  0.6 9.7 %copy-start.3 = (bf16[3,3,64,64]{3,2,1,0:T(8,128)(2,1)S(1)}, bf16[3,3,64,64]{3,2,1,0:T(8,128)(2,1)}, u32[]{:S(2)}) copy-start(bf16[3,3,64,64]{3,2,1,0:T(8,128)(2,1)} %param.10) | copy-start | bytes 221188
  1.7 13.7 %collective-permute-start = (bf16[16,4,8,96]{3,2,1,0:T(8,128)(2,1)S(1)}, bf16[16,4,8,96]{3,2,1,0:T(8,128)(2,1)S(1)}, u32[]{:S(2)}, u32[]{:S(2)}) collective-permute-start(bf16[16,4,8,96]{3,2,1,0:T(8,128)(2,1)S(1)} %get-tuple-element.8), channel_id=1, source_target_pairs={{0,1},{1,2},{2,3},{3,4},{4,5},{5,6},{6,7},{8,9},{9,10},{10,11},{11... | collective-permute-start | bytes 294920 | tf_op jit(solution)/shard_map/ppermute | solution.py:20
  6.3 9.1 %collective-permute-start.1 = (bf16[16,4,8,96]{3,2,1,0:T(8,128)(2,1)S(1)}, bf16[16,4,8,96]{3,2,1,0:T(8,128)(2,1)S(1)}, u32[]{:S(2)}, u32[]{:S(2)}) collective-permute-start(bf16[16,4,8,96]{3,2,1,0:T(8,128)(2,1)S(1)} %get-tuple-element.9), channel_id=1, source_target_pairs={{1,0},{2,1},{3,2},{4,3},{5,4},{6,5},{7,6},{9,8},{10,9},{11,10},{12... | collective-permute-start | bytes 294920 | tf_op jit(solution)/shard_map/ppermute | solution.py:21
  13.8 1.6 %copy-start = (bf16[16,1,32,96,8]{3,4,2,1,0:T(8,128)(2,1)S(1)}, bf16[16,1,32,96,8]{3,4,2,1,0:T(8,128)(2,1)}, u32[]{:S(2)}) copy-start(bf16[16,1,32,96,8]{3,4,2,1,0:T(8,128)(2,1)} %param.6) | copy-start | bytes 2359300
  17.3 9.8 %copy-start.4 = (f32[192]{0:T(256)S(1)}, f32[192]{0:T(256)}, u32[]{:S(2)}) copy-start(f32[192]{0:T(256)} %param.11) | copy-start | bytes 2308
  20.6 8.6 %collective-permute-start.3 = (bf16[16,40,8,4]{1,2,3,0:T(8,128)(2,1)S(1)}, bf16[16,40,8,4]{1,2,3,0:T(8,128)(2,1)S(1)}, u32[]{:S(2)}, u32[]{:S(2)}) collective-permute-start(bf16[16,40,8,4]{1,2,3,0:T(8,128)(2,1)S(1)} %copy.79), channel_id=1, source_target_pairs={{8,0},{16,8},{24,16},{9,1},{17,9},{25,17},{10,2},{18,10},{26,18},{... | collective-permute-start | bytes 122888 | tf_op jit(solution)/shard_map/ppermute | solution.py:26
  21.9 6.4 %collective-permute-start.2 = (bf16[16,40,8,4]{1,2,3,0:T(8,128)(2,1)S(1)}, bf16[16,40,8,4]{1,2,3,0:T(8,128)(2,1)S(1)}, u32[]{:S(2)}, u32[]{:S(2)}) collective-permute-start(bf16[16,40,8,4]{1,2,3,0:T(8,128)(2,1)S(1)} %copy.78), channel_id=1, source_target_pairs={{0,8},{8,16},{16,24},{1,9},{9,17},{17,25},{2,10},{10,18},{18,26},{... | collective-permute-start | bytes 122888 | tf_op jit(solution)/shard_map/ppermute | solution.py:25
  121.4 9.7 %copy-start.1 = (f32[16,128,96]{2,1,0:T(8,128)S(1)}, f32[16,128,96]{2,1,0:T(8,128)}, u32[]{:S(2)}) copy-start(f32[16,128,96]{2,1,0:T(8,128)} %get-tuple-element.5) | copy-start | bytes 2359300

commit v2 on v1

--- a/solution.py
+++ b/solution.py
@@ -14,36 +14,12 @@
 DIRS = ((-1, 0), (1, 0), (0, -1), (0, 1), (-1, -1), (-1, 1), (1, -1), (1, 1))
 
 
-def frames_with_halo(frames, width, n_rows, n_cols):
-    down = [(i, i + 1) for i in range(n_rows - 1)]
-    up = [(i + 1, i) for i in range(n_rows - 1)]
-    above = lax.ppermute(frames[:, -width:], 'rows', down)
-    below = lax.ppermute(frames[:, :width], 'rows', up)
-    tall = jnp.concatenate([above, frames, below], axis=1)
-    right = [(i, i + 1) for i in range(n_cols - 1)]
-    left = [(i + 1, i) for i in range(n_cols - 1)]
-    from_left = lax.ppermute(tall[..., -width:], 'cols', right)
-    from_right = lax.ppermute(tall[..., :width], 'cols', left)
-    return jnp.concatenate([from_left, tall, from_right], axis=-1)
-
-
-def fold_rows(w, order):
-    n_gates = w.shape[-1] // 64
-    blocks = []
-    for rho in order:
-        outs = []
-        for o in range(2):
-            a = rho - o + 1
-            outs.append(w[a] if 0 <= a <= 2 else jnp.zeros_like(w[0]))
-        both = jnp.stack([b.reshape(3, w.shape[2], n_gates, 64) for b in outs], axis=3)
-        blocks.append(both.reshape(3, w.shape[2], n_gates * 128))
-    return jnp.stack(blocks, axis=1)
-
-
-def kernel(dims, x_ref, h_ref, wzr_ref, wn_ref, b_ref, seq_ref, last_ref,
-           hs, rh, zs, xl, stage, row_in, col_in, cor_in, send_sem, recv_sem, out_sem):
+def kernel(dims, x_ref, h_ref, wx_raw, whzr_raw, whn_raw, bias_raw, seq_ref, last_ref,
+           hs, rh, zs, xl, row_in, col_in, cor_in, wzr_ref, wn_ref, wx_ref, b_ref, xs, x_pack, x_row_in, x_col_in,
+           send_sem, recv_sem, x_send_sem, x_recv_sem):
     n_steps, n_pairs, width, n_rows, n_cols = dims
     k = FUSE
+    halo = 2 * k
     first = k + 1
     my_row = lax.axis_index('rows')
     my_col = lax.axis_index('cols')
@@ -53,19 +29,22 @@
         return jnp.logical_and(jnp.logical_and(r >= 0, r < n_rows), jnp.logical_and(c >= 0, c < n_cols))
 
     barrier = pltpu.get_barrier_semaphore()
-    for di, dj in DIRS:
+    def greet(di, dj):
         @pl.when(there(di, dj))
         def _():
             pl.semaphore_signal(barrier, inc=1, device_id={'rows': my_row + di, 'cols': my_col + dj},
                                 device_id_type=pl.DeviceIdType.MESH)
 
+    x_row_in[...] = jnp.zeros_like(x_row_in)
+    x_col_in[...] = jnp.zeros_like(x_col_in)
+    for di, dj in DIRS:
+        greet(di, dj)
     hs[...] = jnp.zeros_like(hs)
     rh[...] = jnp.zeros_like(rh)
+    n_peers = sum(there(di, dj).astype(jnp.int32) for di, dj in DIRS)
+    pl.semaphore_wait(barrier, n_peers)
     for q in range(n_pairs):
         hs[first + q, MARGIN:MARGIN + width, :] = h_ref[q].T
-
-    n_peers = sum(there(di, dj).astype(jnp.int32) for di, dj in DIRS)
-    pl.semaphore_wait(barrier, n_peers)
 
     def src_of(di, dj):
         rows = {-1: pl.ds(first, k), 1: pl.ds(first + n_pairs - k, k), 0: pl.ds(first, n_pairs)}[di]
@@ -116,7 +95,7 @@
         zs[q0:q0 + n] = z.reshape(n, COMP, 128)
         rh[q0:q0 + n, MARGIN - 8:MARGIN - 8 + COMP, :] = r.reshape(n, COMP, 128) * hs[q0:q0 + n, MARGIN - 8:MARGIN - 8 + COMP, :]
 
-    def n_chunk(s, q0, n, slot, last):
+    def n_chunk(s, q0, n, t, last):
         acc = conv(rh, s, q0, n, wn_ref)
         cand = jnp.tanh(acc + b_ref[2:3, :]).reshape(n, COMP, 128)
         h = hs[q0:q0 + n, MARGIN - 8:MARGIN - 8 + COMP, :]
@@ -129,22 +108,111 @@
         for i in range(n):
             q = q0 + i - first
             if 0 <= q < n_pairs:
-                stage[slot, q] = inner[i].T.astype(jnp.bfloat16)
+                seq_ref[t, q] = inner[i].T.astype(jnp.bfloat16)
 
     def chunks(lo, hi):
         for q0 in range(lo, hi, CHUNK):
             yield q0, min(CHUNK, hi - q0)
 
+    n_sub = x_ref.shape[1]
+    edge = halo * 8
+    lane2 = lax.broadcasted_iota(jnp.int32, (1, 128), 1)
+
+    def wide(v):
+        return jnp.concatenate([v, jnp.zeros((v.shape[0], 128 - v.shape[1]), v.dtype)], axis=1)
+
+    def x_copy(d):
+        di, dj = DIRS[d]
+        if dj == 0:
+            src = x_ref.at[:, pl.ds(0 if di < 0 else n_sub - edge, edge), :]
+            dst = x_row_in.at[0 if di < 0 else 1]
+        else:
+            rows = {-1: pl.ds(0, edge), 1: pl.ds(n_sub - edge, edge), 0: pl.ds(0, n_sub)}[di]
+            there_rows = {-1: pl.ds(edge + n_sub, edge), 1: pl.ds(0, edge), 0: pl.ds(edge, n_sub)}[di]
+            side = 0 if dj < 0 else 1
+            src = x_pack.at[side, rows, :]
+            dst = x_col_in.at[side, there_rows, :]
+        return pltpu.make_async_remote_copy(
+            src_ref=src, dst_ref=dst, send_sem=x_send_sem.at[d], recv_sem=x_recv_sem.at[d],
+            device_id={'rows': my_row + di, 'cols': my_col + dj}, device_id_type=pl.DeviceIdType.MESH)
+
+    def pack_x():
+        x_pack[...] = jnp.zeros_like(x_pack)
+
+        def add(t, carry):
+            x = wide(x_ref[t].astype(jnp.float32))
+            here = jnp.logical_and(lane2 >= 8 * t, lane2 < 8 * t + 8)
+            x_pack[0] = jnp.where(here, pltpu.roll(x, 8 * t, 1), x_pack[0].astype(jnp.float32)).astype(jnp.bfloat16)
+            x_pack[1] = jnp.where(here, pltpu.roll(x, lax.rem(8 * t + 128 - (width - 8), 128), 1), x_pack[1].astype(jnp.float32)).astype(jnp.bfloat16)
+            return carry
+        lax.fori_loop(0, n_steps, add, 0)
+
     def build_x(t, s):
-        x = x_ref[t].astype(jnp.float32)
-        taps = (pltpu.roll(x, 1, 1).astype(jnp.bfloat16), x_ref[t], pltpu.roll(x, 127, 1).astype(jnp.bfloat16))
+        lo = lane2 < 8
+        hi = lane2 >= 8 + width
+        for first_sub, n, own, col in ((8, edge, x_row_in[1, t], 0), (8 + edge, n_sub, x_ref[t], edge), (8 + edge + n_sub, edge, x_row_in[0, t], edge + n_sub)):
+            v = pltpu.roll(wide(own.astype(jnp.float32)), 8, 1)
+            from_left = pltpu.roll(x_col_in[1, col:col + n, :].astype(jnp.float32), lax.rem(128 - 8 * t, 128), 1)
+            from_right = pltpu.roll(x_col_in[0, col:col + n, :].astype(jnp.float32), lax.rem(128 + 8 + width - 8 * t, 128), 1)
+            v = jnp.where(lo, from_left, jnp.where(hi, from_right, v))
+            xs[0, first_sub:first_sub + n, :] = pltpu.roll(v, 1, 1)
+            xs[1, first_sub:first_sub + n, :] = v
+            xs[2, first_sub:first_sub + n, :] = pltpu.roll(v, 127, 1)
         zero = jnp.zeros((32, 128), jnp.bfloat16)
         for i in range(n_pairs + 2 * k):
-            both = jnp.concatenate([tap[16 * i:16 * i + 32] for tap in taps] + [zero], axis=0)
+            both = jnp.concatenate([xs[c, 16 * i:16 * i + 32].astype(jnp.bfloat16) for c in range(3)] + [zero], axis=0)
             xl[s, i] = both.T[:COMP]
 
-    def out_copy(t, slot):
-        return pltpu.make_async_copy(stage.at[slot], seq_ref.at[t], out_sem.at[slot])
+    def fold_weights():
+        def pair(get, a0, a1, gate):
+            lo_part = get(a0, gate, 0) if 0 <= a0 <= 2 else None
+            hi_part = get(a1, gate, 1) if 0 <= a1 <= 2 else None
+            zero = jnp.zeros_like(lo_part if hi_part is None else hi_part)
+            return jnp.where(lane2 < 64, zero if lo_part is None else lo_part, zero if hi_part is None else hi_part)
+
+        for c in range(3):
+            def get_h(a, gate, high):
+                if gate == 2:
+                    v = wide(whn_raw[a, c].astype(jnp.float32))
+                    return pltpu.roll(v, 64, 1) if high else v
+                v = whzr_raw[a, c].astype(jnp.float32)
+                return pltpu.roll(v, 64, 1) if high != gate else v
+
+            def get_x(a, gate, high):
+                v = wx_raw[a, c].astype(jnp.float32)
+                v = wide(v[:, 128:]) if gate == 2 else v[:, :128]
+                return pltpu.roll(v, 64, 1) if high != (gate % 2) else v
+
+            for j, rho in enumerate((0, 1, 2, -1)):
+                at = c * 256 + j * 64
+                for gate in range(2):
+                    wzr_ref[at:at + 64, gate * 128:gate * 128 + 128] = pair(get_h, rho + 1, rho, gate).astype(jnp.bfloat16)
+                wn_ref[at:at + 64, :] = pair(get_h, rho + 1, rho, 2).astype(jnp.bfloat16)
+            for j, rho in enumerate((-1, 0, 1, 2)):
+                at = c * 32 + j * 8
+                for gate in range(3):
+                    wx_ref[at:at + 8, gate * 128:gate * 128 + 128] = pair(get_x, rho + 1, rho, gate)
+        wx_ref[96:128, :] = jnp.zeros((32, 384), jnp.float32)
+        wzr_ref[768:896, :] = wx_ref[:, :256].astype(jnp.bfloat16)
+        wn_ref[768:896, :] = wx_ref[:, 256:].astype(jnp.bfloat16)
+        zr = bias_raw[:, :128]
+        turned = pltpu.roll(zr, 64, 1)
+        cand = wide(bias_raw[:, 128:])
+        b_ref[0:1, :] = jnp.where(lane2 < 64, zr, turned)
+        b_ref[1:2, :] = jnp.where(lane2 < 64, turned, zr)
+        b_ref[2:3, :] = jnp.where(lane2 < 64, cand, pltpu.roll(cand, 64, 1))
+
+    pack_x()
+    for d, (di, dj) in enumerate(DIRS):
+        @pl.when(there(di, dj))
+        def _():
+            x_copy(d).start()
+    fold_weights()
+    xs[...] = jnp.zeros_like(xs)
+    for d, (di, dj) in enumerate(DIRS):
+        @pl.when(there(-di, -dj))
+        def _():
+            x_copy(d).wait_recv()
 
     def period(p, carry):
         par = lax.rem(p, 2)
@@ -163,7 +231,6 @@
         for s in range(k):
             ext = k - 1 - s
             t = p * k + s
-            slot = s % 2 if k % 2 == 0 else lax.rem(t, 2)
             for q0, n in chunks(first - ext - 1, first + n_pairs + ext + 1):
                 zr_chunk(s, q0, n)
             if s == 0:
@@ -172,12 +239,8 @@
                     def _():
                         copy_of(d, par).wait_send()
 
-            @pl.when(t >= 2)
-            def _():
-                out_copy(t - 2, slot).wait()
             for q0, n in chunks(first - ext, first + n_pairs + ext):
-                n_chunk(s, q0, n, slot, s == k - 1)
-            out_copy(t, slot).start()
+                n_chunk(s, q0, n, t, s == k - 1)
             if s < k - 1:
                 @pl.when(my_row == 0)
                 def _():
@@ -199,8 +262,10 @@
     lax.fori_loop(0, n_steps // k, period, 0)
     for q in range(n_pairs):
         last_ref[q] = hs[first + q, MARGIN:MARGIN + width, :].T
-    for t in range(n_steps - 2, n_steps):
-        out_copy(t, t % 2).wait()
+    for d, (di, dj) in enumerate(DIRS):
+        @pl.when(there(di, dj))
+        def _():
+            x_copy(d).wait_send()
 
 
 def solution(mesh):
@@ -214,39 +279,40 @@
         n_hidden = h_init.shape[-1]
         k = FUSE
         n_pairs = tile_h // 2
-        halo = 2 * k
-        x = frames_with_halo(frames[:, 0].transpose(0, 1, 3, 2), halo, n_rows, n_cols)
-        x = jnp.pad(x, ((0, 0), (1, 1), (0, 0), (8 - halo, 128 - 8 - width - halo)))
-        x = x.reshape(n_steps, (tile_h + 2 * halo + 2) * c_in, 128)
+        x = frames[:, 0].transpose(0, 1, 3, 2).reshape(n_steps, tile_h * c_in, width)
         h0 = h_init[0].transpose(0, 2, 1).reshape(n_pairs, 2 * n_hidden, width)
-        wx = fold_rows(w_x, (-1, 0, 1, 2)).reshape(96, 384)
-        wx = jnp.pad(wx, ((0, 32), (0, 0)))
-        wzr = jnp.concatenate([fold_rows(w_hzr, (0, 1, 2, -1)).reshape(768, 256), wx[:, :256]], axis=0)
-        wn = jnp.concatenate([fold_rows(w_hn, (0, 1, 2, -1)).reshape(768, 128), wx[:, 256:]], axis=0)
-        bias = jnp.tile(gate_bias.reshape(3, 1, n_hidden), (1, 2, 1)).reshape(3, 128)
+        edge = 2 * k * c_in
         n_buf = n_pairs + 2 * k + 2
         vmem = pl.BlockSpec(memory_space=pltpu.VMEM)
         seq, last = pl.pallas_call(
             functools.partial(kernel, (n_steps, n_pairs, width, n_rows, n_cols)),
-            out_shape=(jax.ShapeDtypeStruct((n_steps, n_pairs, 128, width), jnp.bfloat16),
+            out_shape=(pltpu.VMEM((n_steps, n_pairs, 128, width), jnp.bfloat16),
                        jax.ShapeDtypeStruct((n_pairs, 128, width), jnp.float32)),
-            in_specs=[vmem] * 5,
-            out_specs=(pl.BlockSpec(memory_space=pl.ANY), vmem),
+            in_specs=[vmem] * 6,
+            out_specs=(vmem, vmem),
             scratch_shapes=[
                 pltpu.VMEM((n_buf, 128, 128), jnp.float32),
                 pltpu.VMEM((n_buf, 128, 128), jnp.float32),
                 pltpu.VMEM((n_buf, COMP, 128), jnp.float32),
                 pltpu.VMEM((k, n_pairs + 2 * k, COMP, 128), jnp.bfloat16),
-                pltpu.VMEM((2, n_pairs, 128, width), jnp.bfloat16),
                 pltpu.VMEM((2, 2, k, width, 128), jnp.float32),
                 pltpu.VMEM((2, 2, n_pairs, 8, 128), jnp.float32),
                 pltpu.VMEM((2, 4, k, 8, 128), jnp.float32),
+                pltpu.VMEM((896, 256), jnp.bfloat16),
+                pltpu.VMEM((896, 128), jnp.bfloat16),
+                pltpu.VMEM((128, 384), jnp.float32),
+                pltpu.VMEM((3, 128), jnp.float32),
+                pltpu.VMEM((3, tile_h * c_in + 2 * edge + 16, 128), jnp.float32),
+                pltpu.VMEM((2, tile_h * c_in, 128), jnp.bfloat16),
+                pltpu.VMEM((2, n_steps, edge, width), jnp.bfloat16),
+                pltpu.VMEM((2, tile_h * c_in + 2 * edge, 128), jnp.bfloat16),
                 pltpu.SemaphoreType.DMA((8,)),
                 pltpu.SemaphoreType.DMA((2, 8)),
-                pltpu.SemaphoreType.DMA((2,)),
+                pltpu.SemaphoreType.DMA((8,)),
+                pltpu.SemaphoreType.DMA((8,)),
             ],
-            compiler_params=pltpu.CompilerParams(collective_id=0, has_side_effects=True),
-        )(x, h0, wzr, wn, bias)
+            compiler_params=pltpu.CompilerParams(collective_id=0, has_side_effects=True, vmem_limit_bytes=32 * 2**20),
+        )(x, h0, w_x, w_hzr, w_hn, gate_bias.reshape(1, -1))
         seq = seq.reshape(n_steps, 1, tile_h, n_hidden, width).transpose(0, 1, 2, 4, 3)
         last = last.reshape(1, tile_h, n_hidden, width).transpose(0, 1, 3, 2)
         return seq, last

time: 132 us -> 98.4 us (0.75)
  local copies, waits for them, and re-layouts: 25.5 us -> 10.1 us
  starting transfers between devices: 12.3 us -> 0 us
  other arithmetic: 6.57 us -> 0 us
    ppermute x4 -> x0, starting transfers between devices: 12.3 us -> none  [the longest x1 4.6 us: frames_with_halo(): above = lax.ppermute(frames[:, -width:], 'rows', down)]
    another operation x36 -> x0, local copies, waits for them, and re-layouts: 4.56 us -> none  [the longest x19 2.31 us: fold_rows(): jnp.stack([b.reshape(3, w.shape[2], n_gates, 64) for b in outs], axis=3)]
    unnamed x20 -> x14, local copies, waits for them, and re-layouts: 14.6 us -> 10.1 us
    reshape x1 -> x0, other arithmetic: 4.01 us -> none  [local_fn(): x = x.reshape(n_steps, (tile_h + 2 * halo + 2) * c_in, 128)]
    slice x6 -> x0, local copies, waits for them, and re-layouts: 3.41 us -> none  [the longest x1 1.61 us: frames_with_halo(): from_left = lax.ppermute(tall[..., -width:], 'cols', right)]
    ppermute x2 -> x0, local copies, waits for them, and re-layouts: 2.89 us -> none  [the longest x1 1.96 us: frames_with_halo(): from_right = lax.ppermute(tall[..., :width], 'cols', left)]
    concatenate x3 -> x0, other arithmetic: 1.82 us -> none  [the longest x1 0.8 us: local_fn(): jnp.concatenate([fold_rows(w_hzr, (0, 1, 2, -1)).reshape(768, 256), wx[:,...]
  transfers between devices with their start and end apart: 4 -> 0, of which waited for: 1 -> 0; matrix products, arithmetic and copies ran while one was open for 7% -> 0% of each run, Pallas kernels for 0% -> 0%
where the time goes in v2:
time: 98.4 us; the launch traced here: 98.1 us
  Pallas kernels  87.3 us (89%)
  local copies, waits for them, and re-layouts  10.1 us (10%)
    pallas_call x1, Pallas kernels, local_fn(): pl.pallas_call(functools.partial(kernel, (n_steps, n_pairs, width, n_rows...  87.3 us
    unnamed x14, local copies, waits for them, and re-layouts  10.1 us

profile of v2, /device:TPU:97, one launch (start us, length us, event | category | flops | bytes accessed | tf_op | source)
XLA Modules:
  0.0 98.1 jit_solution(17440586665721935677)
XLA Ops:
  0.6 0.0 copy-start
  0.6 1.2 %copy-done = bf16[16,1,32,96,8]{3,4,2,1,0:T(8,128)(2,1)S(1)} copy-done((bf16[16,1,32,96,8]{3,4,2,1,0:T(8,128)(2,1)S(1)}, bf16[16,1,32,96,8]{3,4,2,1,0:T(8,128)(2,1)}, u32[]{:S(2)}) %copy-start) | copy-done | bytes 786456
  1.9 0.0 copy-start.1
  1.9 1.2 %copy-done.1 = f32[1,32,96,64]{2,3,1,0:T(8,128)S(1)} copy-done((f32[1,32,96,64]{2,3,1,0:T(8,128)S(1)}, f32[1,32,96,64]{2,3,1,0:T(8,128)}, u32[]{:S(2)}) %copy-start.1) | copy-done | bytes 786456
  3.1 0.0 copy-start.2
  3.1 0.9 copy-done.2
  4.0 0.0 copy-start.3
  4.0 0.9 copy-done.3
  4.9 0.0 copy-start.4
  4.9 0.8 copy-done.4
  5.7 0.0 copy-start.5
  5.7 0.7 copy-done.5
  6.4 87.3 %shard_map.77 = (bf16[16,16,128,96]{3,2,1,0:T(8,128)(2,1)S(1)}, f32[16,128,96]{2,1,0:T(8,128)S(1)}) custom-call(bf16[16,256,96]{2,1,0:T(8,128)(2,1)S(1)} %bitcast.20, f32[16,128,96]{2,1,0:T(8,128)S(1)} %bitcast.21, bf16[3,3,8,192]{3,2,1,0:T(8,128)(2,1)S(1)} %copy-done.4, bf16[3,3,64,128]{3,2,1,0:T(8,128)(2,1)S(1)} %copy-done.2, ...), custom_call_target="tpu_custom_call" | custom-call | tf_op jit(solution)/shard_map/pallas_call | solution.py:287
  93.7 3.4 %copy.11 = bf16[16,1,32,96,64]{3,4,2,1,0:T(8,128)(2,1)} copy(bf16[16,1,32,96,64]{3,4,2,1,0:T(8,128)(2,1)S(1)} %bitcast.19) | data formatting | bytes 12582912
  97.1 1.0 copy.12
Async XLA Ops:
  0.6 1.2 %copy-start = (bf16[16,1,32,96,8]{3,4,2,1,0:T(8,128)(2,1)S(1)}, bf16[16,1,32,96,8]{3,4,2,1,0:T(8,128)(2,1)}, u32[]{:S(2)}) copy-start(bf16[16,1,32,96,8]{3,4,2,1,0:T(8,128)(2,1)} %param.6) | copy-start | bytes 2359300
  1.9 1.2 %copy-start.1 = (f32[1,32,96,64]{2,3,1,0:T(8,128)S(1)}, f32[1,32,96,64]{2,3,1,0:T(8,128)}, u32[]{:S(2)}) copy-start(f32[1,32,96,64]{2,3,1,0:T(8,128)} %param.7) | copy-start | bytes 2359300
  3.1 0.9 copy-start.2
  4.0 0.9 copy-start.3
  4.9 0.8 copy-start.4
  5.7 0.7 copy-start.5

commit v3 on v2

--- a/solution.py
+++ b/solution.py
@@ -8,15 +8,16 @@
 from jax.sharding import PartitionSpec as P
 
 FUSE = 2
-CHUNK = 4
+CHUNK = 2
 MARGIN = 16
 COMP = 112
 DIRS = ((-1, 0), (1, 0), (0, -1), (0, 1), (-1, -1), (-1, 1), (1, -1), (1, 1))
 
 
-def kernel(dims, x_ref, h_ref, wx_raw, whzr_raw, whn_raw, bias_raw, seq_ref, last_ref,
+def kernel(dims, x_hbm, h_hbm, wx_hbm, whzr_hbm, whn_hbm, bias_hbm, seq_ref, last_ref,
+           x_ref, h_ref, wx_raw, whzr_raw, whn_raw, bias_raw,
            hs, rh, zs, xl, row_in, col_in, cor_in, wzr_ref, wn_ref, wx_ref, b_ref, xs, x_pack, x_row_in, x_col_in,
-           send_sem, recv_sem, x_send_sem, x_recv_sem):
+           send_sem, recv_sem, x_send_sem, x_recv_sem, load_sem):
     n_steps, n_pairs, width, n_rows, n_cols = dims
     k = FUSE
     halo = 2 * k
@@ -28,6 +29,10 @@
         r, c = my_row + di, my_col + dj
         return jnp.logical_and(jnp.logical_and(r >= 0, r < n_rows), jnp.logical_and(c >= 0, c < n_cols))
 
+    loads = [pltpu.make_async_copy(src, dst, load_sem.at[i]) for i, (src, dst) in enumerate(
+        ((x_hbm, x_ref), (h_hbm, h_ref), (wx_hbm, wx_raw), (whzr_hbm, whzr_raw), (whn_hbm, whn_raw), (bias_hbm, bias_raw)))]
+    for load in loads:
+        load.start()
     barrier = pltpu.get_barrier_semaphore()
     def greet(di, dj):
         @pl.when(there(di, dj))
@@ -43,33 +48,41 @@
     rh[...] = jnp.zeros_like(rh)
     n_peers = sum(there(di, dj).astype(jnp.int32) for di, dj in DIRS)
     pl.semaphore_wait(barrier, n_peers)
-    for q in range(n_pairs):
-        hs[first + q, MARGIN:MARGIN + width, :] = h_ref[q].T
-
-    def src_of(di, dj):
-        rows = {-1: pl.ds(first, k), 1: pl.ds(first + n_pairs - k, k), 0: pl.ds(first, n_pairs)}[di]
-        cols = {-1: pl.ds(MARGIN, 8), 1: pl.ds(MARGIN + width - 8, 8), 0: pl.ds(MARGIN, width)}[dj]
-        return rows, cols
-
-    def dst_of(di, dj):
-        rows = {-1: pl.ds(first + n_pairs, k), 1: pl.ds(first - k, k), 0: pl.ds(first, n_pairs)}[di]
-        cols = {-1: pl.ds(MARGIN + width, 8), 1: pl.ds(MARGIN - 8, 8), 0: pl.ds(MARGIN, width)}[dj]
-        return rows, cols
-
-    def landing(d, par):
-        if d < 2:
-            return row_in.at[par, d]
-        if d < 4:
-            return col_in.at[par, d - 2]
-        return cor_in.at[par, d - 4]
-
-    def copy_of(d, par):
-        di, dj = DIRS[d]
-        rows, cols = src_of(di, dj)
-        return pltpu.make_async_remote_copy(
-            src_ref=hs.at[rows, cols, :], dst_ref=landing(d, par), send_sem=send_sem.at[d],
-            recv_sem=recv_sem.at[par, d], device_id={'rows': my_row + di, 'cols': my_col + dj},
-            device_id_type=pl.DeviceIdType.MESH)
+    moves = [(-1, 0, 0), (1, 0, 0)] + [(di, dj, 0) for di in (-1, 1) for dj in (-1, 1)]
+    group = n_pairs // 4
+    moves += [(0, dj, g) for g in range(4) for dj in (-1, 1)]
+    sent_with = {0: (0, 2, 3, 6, 7), 1: (8, 9), 2: (10, 11), 3: (1, 4, 5, 12, 13)}
+
+    def move(m, par):
+        di, dj, g = moves[m]
+        cols = {-1: pl.ds(MARGIN, halo), 1: pl.ds(MARGIN + width - halo, halo), 0: pl.ds(MARGIN, width)}[dj]
+        if di == 0:
+            src = hs.at[pl.ds(first + g * group, group), cols, :]
+            dst = col_in.at[par, (dj + 1) // 2, pl.ds(g * group, group)]
+        else:
+            src = hs.at[pl.ds(first if di < 0 else first + n_pairs - k, k), cols, :]
+            dst = row_in.at[par, (di + 1) // 2] if dj == 0 else cor_in.at[par, m - 2]
+        return dst, pltpu.make_async_remote_copy(
+            src_ref=src, dst_ref=dst, send_sem=send_sem.at[m], recv_sem=recv_sem.at[par, m],
+            device_id={'rows': my_row + di, 'cols': my_col + dj}, device_id_type=pl.DeviceIdType.MESH)
+
+    def send(g, par):
+        for m in sent_with[g]:
+            @pl.when(there(moves[m][0], moves[m][1]))
+            def _():
+                move(m, par)[1].start()
+
+    def receive(g, par):
+        for m in sent_with[g]:
+            di, dj, _ = moves[m]
+
+            @pl.when(there(-di, -dj))
+            def _():
+                dst, copy = move(m, par)
+                copy.wait_recv()
+                cols = {-1: pl.ds(MARGIN + width, halo), 1: pl.ds(MARGIN - halo, halo), 0: pl.ds(MARGIN, width)}[dj]
+                rows = pl.ds(first + g * group, group) if di == 0 else pl.ds(first + n_pairs if di < 0 else first - k, k)
+                hs[rows, cols, :] = dst[...]
 
     lane = lax.broadcasted_iota(jnp.int32, (1, 1, 128), 2)
     low = lane < 64
@@ -202,11 +215,19 @@
         b_ref[1:2, :] = jnp.where(lane2 < 64, turned, zr)
         b_ref[2:3, :] = jnp.where(lane2 < 64, cand, pltpu.roll(cand, 64, 1))
 
+    loads[0].wait()
     pack_x()
     for d, (di, dj) in enumerate(DIRS):
         @pl.when(there(di, dj))
         def _():
             x_copy(d).start()
+    loads[1].wait()
+    for q in range(n_pairs):
+        hs[first + q, MARGIN:MARGIN + width, :] = h_ref[q].T
+    for g in (0, 3, 1, 2):
+        send(g, 0)
+    for load in loads[2:]:
+        load.wait()
     fold_weights()
     xs[...] = jnp.zeros_like(xs)
     for d, (di, dj) in enumerate(DIRS):
@@ -214,34 +235,41 @@
         def _():
             x_copy(d).wait_recv()
 
+    def zr(s, lo, hi):
+        for q0, n in chunks(first + lo, first + hi):
+            zr_chunk(s, q0, n)
+
+    def cand(t, s, lo, hi):
+        for q0, n in chunks(first + lo, first + hi):
+            n_chunk(s, q0, n, t, s == k - 1)
+
+    n_periods = n_steps // k
+
     def period(p, carry):
         par = lax.rem(p, 2)
-        for d, (di, dj) in enumerate(DIRS):
-            @pl.when(there(di, dj))
-            def _():
-                copy_of(d, par).start()
         for s in range(k):
             build_x(p * k + s, s)
-        for d, (di, dj) in enumerate(DIRS):
-            @pl.when(there(-di, -dj))
-            def _():
-                copy_of(d, par).wait_recv()
-                rows, cols = dst_of(di, dj)
-                hs[rows, cols, :] = landing(d, par)[...]
         for s in range(k):
             ext = k - 1 - s
             t = p * k + s
-            for q0, n in chunks(first - ext - 1, first + n_pairs + ext + 1):
-                zr_chunk(s, q0, n)
             if s == 0:
-                for d, (di, dj) in enumerate(DIRS):
+                receive(0, par)
+                receive(3, par)
+                zr(s, -ext - 1, group - 1)
+                zr(s, 3 * group + 1, n_pairs + ext + 1)
+                receive(1, par)
+                zr(s, group - 1, 2 * group - 1)
+                receive(2, par)
+                zr(s, 2 * group - 1, 3 * group + 1)
+                for m, (di, dj, _) in enumerate(moves):
                     @pl.when(there(di, dj))
                     def _():
-                        copy_of(d, par).wait_send()
-
-            for q0, n in chunks(first - ext, first + n_pairs + ext):
-                n_chunk(s, q0, n, t, s == k - 1)
+                        move(m, par)[1].wait_send()
             if s < k - 1:
+                if s > 0:
+                    zr(s, -ext - 1, n_pairs + ext + 1)
+                cand(t, s, -ext, n_pairs + ext)
+
                 @pl.when(my_row == 0)
                 def _():
                     hs[first - ext:first, :, :] = jnp.zeros((ext, 128, 128), jnp.float32)
@@ -257,6 +285,26 @@
                 @pl.when(my_col == n_cols - 1)
                 def _():
                     hs[:, MARGIN + width:MARGIN + width + 8, :] = jnp.zeros((hs.shape[0], 8, 128), jnp.float32)
+            else:
+                more = p + 1 < n_periods
+
+                def send_next(g):
+                    @pl.when(more)
+                    def _():
+                        send(g, 1 - par)
+                if s > 0:
+                    zr(s, -1, group + 1)
+                    zr(s, 3 * group - 1, n_pairs + 1)
+                cand(t, s, 0, group)
+                send_next(0)
+                cand(t, s, 3 * group, n_pairs)
+                send_next(3)
+                if s > 0:
+                    zr(s, group + 1, 3 * group - 1)
+                cand(t, s, group, 2 * group)
+                send_next(1)
+                cand(t, s, 2 * group, 3 * group)
+                send_next(2)
         return carry
 
     lax.fori_loop(0, n_steps // k, period, 0)
@@ -288,16 +336,22 @@
             functools.partial(kernel, (n_steps, n_pairs, width, n_rows, n_cols)),
             out_shape=(pltpu.VMEM((n_steps, n_pairs, 128, width), jnp.bfloat16),
                        jax.ShapeDtypeStruct((n_pairs, 128, width), jnp.float32)),
-            in_specs=[vmem] * 6,
+            in_specs=[pl.BlockSpec(memory_space=pltpu.HBM)] * 6,
             out_specs=(vmem, vmem),
             scratch_shapes=[
+                pltpu.VMEM(x.shape, x.dtype),
+                pltpu.VMEM(h0.shape, h0.dtype),
+                pltpu.VMEM(w_x.shape, w_x.dtype),
+                pltpu.VMEM(w_hzr.shape, w_hzr.dtype),
+                pltpu.VMEM(w_hn.shape, w_hn.dtype),
+                pltpu.VMEM((1, gate_bias.shape[0]), gate_bias.dtype),
                 pltpu.VMEM((n_buf, 128, 128), jnp.float32),
                 pltpu.VMEM((n_buf, 128, 128), jnp.float32),
                 pltpu.VMEM((n_buf, COMP, 128), jnp.float32),
                 pltpu.VMEM((k, n_pairs + 2 * k, COMP, 128), jnp.bfloat16),
                 pltpu.VMEM((2, 2, k, width, 128), jnp.float32),
-                pltpu.VMEM((2, 2, n_pairs, 8, 128), jnp.float32),
-                pltpu.VMEM((2, 4, k, 8, 128), jnp.float32),
+                pltpu.VMEM((2, 2, n_pairs, 2 * k, 128), jnp.float32),
+                pltpu.VMEM((2, 4, k, 2 * k, 128), jnp.float32),
                 pltpu.VMEM((896, 256), jnp.bfloat16),
                 pltpu.VMEM((896, 128), jnp.bfloat16),
                 pltpu.VMEM((128, 384), jnp.float32),
@@ -306,13 +360,14 @@
                 pltpu.VMEM((2, tile_h * c_in, 128), jnp.bfloat16),
                 pltpu.VMEM((2, n_steps, edge, width), jnp.bfloat16),
                 pltpu.VMEM((2, tile_h * c_in + 2 * edge, 128), jnp.bfloat16),
-                pltpu.SemaphoreType.DMA((8,)),
-                pltpu.SemaphoreType.DMA((2, 8)),
+                pltpu.SemaphoreType.DMA((14,)),
+                pltpu.SemaphoreType.DMA((2, 14)),
                 pltpu.SemaphoreType.DMA((8,)),
                 pltpu.SemaphoreType.DMA((8,)),
+                pltpu.SemaphoreType.DMA((6,)),
             ],
             compiler_params=pltpu.CompilerParams(collective_id=0, has_side_effects=True, vmem_limit_bytes=32 * 2**20),
-        )(x, h0, w_x, w_hzr, w_hn, gate_bias.reshape(1, -1))
+        )(*[pltpu.with_memory_space_constraint(v, pltpu.HBM) for v in (x, h0, w_x, w_hzr, w_hn, gate_bias.reshape(1, -1))])
         seq = seq.reshape(n_steps, 1, tile_h, n_hidden, width).transpose(0, 1, 2, 4, 3)
         last = last.reshape(1, tile_h, n_hidden, width).transpose(0, 1, 3, 2)
         return seq, last

time: 98.4 us -> 85.3 us (0.87)
  Pallas kernels: 87.3 us -> 80.2 us
  local copies, waits for them, and re-layouts: 10.1 us -> 4.37 us
    pallas_call x1, Pallas kernels: 87.3 us -> 80.2 us  [local_fn(): pl.pallas_call(functools.partial(kernel, (n_steps, n_pairs, width, n_rows...]
    unnamed x14 -> x2, local copies, waits for them, and re-layouts: 10.1 us -> 4.37 us
where the time goes in v3:
time: 85.3 us; the launch traced here: 85.2 us
  Pallas kernels  80.2 us (94%)
  local copies, waits for them, and re-layouts  4.37 us (5%)
    pallas_call x1, Pallas kernels, local_fn(): pl.pallas_call(functools.partial(kernel, (n_steps, n_pairs, width, n_rows...  80.2 us
    unnamed x2, local copies, waits for them, and re-layouts  4.37 us

profile of v3, /device:TPU:97, one launch (start us, length us, event | category | flops | bytes accessed | tf_op | source)
XLA Modules:
  0.0 85.2 jit_solution(7582863984295907157)
XLA Ops:
  0.6 80.2 %shard_map.77 = (bf16[16,16,128,96]{3,2,1,0:T(8,128)(2,1)S(1)}, f32[16,128,96]{2,1,0:T(8,128)S(1)}) custom-call(bf16[16,256,96]{2,1,0:T(8,128)(2,1)} %bitcast.21, f32[16,128,96]{2,1,0:T(8,128)} %bitcast.22, bf16[3,3,8,192]{3,2,1,0:T(8,128)(2,1)} %wx_hbm.1, bf16[3,3,64,128]{3,2,1,0:T(8,128)(2,1)} %whzr_hbm.1, bf16[3,3,64,64]{3,2,1,0:T(8,128)(2,1)} %whn_hbm.1, ...), custom_call_target="tpu_custom_call" | custom-call | tf_op jit(solution)/shard_map/pallas_call | solution.py:335
  80.8 3.4 %copy.11 = bf16[16,1,32,96,64]{3,4,2,1,0:T(8,128)(2,1)} copy(bf16[16,1,32,96,64]{3,4,2,1,0:T(8,128)(2,1)S(1)} %bitcast.19) | data formatting | bytes 12582912
  84.2 1.0 %copy.12 = f32[1,32,96,64]{2,3,1,0:T(8,128)} copy(f32[1,32,96,64]{2,3,1,0:T(8,128)S(1)} %bitcast.20) | data formatting | bytes 1572864

commit v4 on v3

v4 whole, which is shorter than its diff:
```python
import functools

import jax
import jax.numpy as jnp
from jax import lax
from jax.experimental import pallas as pl
from jax.experimental.pallas import tpu as pltpu
from jax.sharding import PartitionSpec as P

FUSE = 2
CHUNK = 2
N_CHUNK = 2
RIM = 4
MARGIN = 16
COMP = 112
DIRS = ((-1, 0), (1, 0), (0, -1), (0, 1), (-1, -1), (-1, 1), (1, -1), (1, 1))


def kernel(dims, x_hbm, h_hbm, wx_hbm, whzr_hbm, whn_hbm, bias_hbm, seq_ref, last_ref,
           x_ref, h_ref, wx_raw, whzr_raw, whn_raw, bias_raw,
           hs, rh, zs, xl, gate_zr, gate_n, row_in, col_in, cor_in, wzr_ref, wn_ref, wx_ref, wxzr_ref, wxn_ref, b_ref, xs, x_pack, x_row_in, x_col_in,
           send_sem, recv_sem, x_send_sem, x_recv_sem, load_sem):
    n_steps, n_pairs, width, n_rows, n_cols = dims
    k = FUSE
    halo = 2 * k
    first = k + 1
    my_row = lax.axis_index('rows')
    my_col = lax.axis_index('cols')

    def there(di, dj):
        r, c = my_row + di, my_col + dj
        return jnp.logical_and(jnp.logical_and(r >= 0, r < n_rows), jnp.logical_and(c >= 0, c < n_cols))

    loads = [pltpu.make_async_copy(src, dst, load_sem.at[i]) for i, (src, dst) in enumerate(
        ((x_hbm, x_ref), (h_hbm, h_ref), (wx_hbm, wx_raw), (whzr_hbm, whzr_raw), (whn_hbm, whn_raw), (bias_hbm, bias_raw)))]
    for load in loads:
        load.start()
    barrier = pltpu.get_barrier_semaphore()
    def device(di, dj):
        return (lax.axis_index('batch') * n_cols + my_col + dj) * n_rows + my_row + di

    def greet(di, dj):
        @pl.when(there(di, dj))
        def _():
            pl.semaphore_signal(barrier, inc=1, device_id=device(di, dj),
                                device_id_type=pl.DeviceIdType.LOGICAL)

    x_row_in[...] = jnp.zeros_like(x_row_in)
    x_col_in[...] = jnp.zeros_like(x_col_in)
    row_in[...] = jnp.zeros_like(row_in)
    col_in[...] = jnp.zeros_like(col_in)
    cor_in[...] = jnp.zeros_like(cor_in)
    for di, dj in DIRS:
        greet(di, dj)
    hs[...] = jnp.zeros_like(hs)
    rh[...] = jnp.zeros_like(rh)
    n_peers = sum(there(di, dj).astype(jnp.int32) for di, dj in DIRS)
    pl.semaphore_wait(barrier, n_peers)
    moves = [(-1, 0, 0), (1, 0, 0)] + [(di, dj, 0) for di in (-1, 1) for dj in (-1, 1)]
    bounds = ((0, RIM), (RIM, n_pairs - RIM), (n_pairs - RIM, n_pairs))
    moves += [(0, dj, g) for g in range(3) for dj in (-1, 1)]
    rim = (0, 1, 2, 3, 4, 5, 6, 7, 10, 11)
    middle = (8, 9)

    def landing(m, par):
        di, dj, g = moves[m]
        if di == 0:
            return col_in.at[par, (dj + 1) // 2, pl.ds(bounds[g][0], bounds[g][1] - bounds[g][0])]
        return row_in.at[par, (di + 1) // 2] if dj == 0 else cor_in.at[par, m - 2]

    def move(m, par):
        di, dj, g = moves[m]
        cols = {-1: pl.ds(MARGIN, halo), 1: pl.ds(MARGIN + width - halo, halo), 0: pl.ds(MARGIN, width)}[dj]
        if di == 0:
            rows = pl.ds(first + bounds[g][0], bounds[g][1] - bounds[g][0])
        else:
            rows = pl.ds(first if di < 0 else first + n_pairs - k, k)
        return pltpu.make_async_remote_copy(
            src_ref=hs.at[rows, cols, :], dst_ref=landing(m, par), send_sem=send_sem.at[m], recv_sem=recv_sem.at[par, m],
            device_id=device(di, dj), device_id_type=pl.DeviceIdType.LOGICAL)

    def send(which, par):
        for m in which:
            @pl.when(there(moves[m][0], moves[m][1]))
            def _():
                move(m, par).start()

    def receive(which, par):
        for m in which:
            @pl.when(there(-moves[m][0], -moves[m][1]))
            def _():
                move(m, par).wait_recv()
        for m in which:
            di, dj, g = moves[m]
            cols = {-1: pl.ds(MARGIN + width, halo), 1: pl.ds(MARGIN - halo, halo), 0: pl.ds(MARGIN, width)}[dj]
            if di == 0:
                rows = pl.ds(first + bounds[g][0], bounds[g][1] - bounds[g][0])
            else:
                rows = pl.ds(first + n_pairs if di < 0 else first - k, k)
            hs[rows, cols, :] = landing(m, par)[...]

    lane = lax.broadcasted_iota(jnp.int32, (1, 1, 128), 2)
    low = lane < 64

    def conv_zr(q0, n):
        parts = []
        for c in range(3):
            cols = pl.ds(MARGIN - 9 + c, COMP)
            own = hs[q0:q0 + n, cols, :]
            edge = jnp.where(low, hs[q0 + 1:q0 + 1 + n, cols, :], hs[q0 - 1:q0 - 1 + n, cols, :])
            parts += [own.astype(jnp.bfloat16), edge.astype(jnp.bfloat16)]
        lhs = jnp.concatenate(parts, axis=-1).reshape(n * COMP, 6 * 128)
        return jnp.dot(lhs, wzr_ref[...], preferred_element_type=jnp.float32)

    def conv_n(q0, n):
        parts = []
        for c in range(3):
            cols = pl.ds(MARGIN - 9 + c, COMP)
            own = rh[q0:q0 + n, cols, :].astype(jnp.bfloat16).reshape(n // 2, 2, COMP, 128)
            edge = jnp.stack([jnp.where(low[0], rh[q + 2, cols, :], rh[q - 1, cols, :]).astype(jnp.bfloat16) for q in range(q0, q0 + n, 2)])
            parts += [own[:, 0], own[:, 1], edge]
        lhs = jnp.concatenate(parts, axis=-1).reshape(n // 2 * COMP, 9 * 128)
        return jnp.dot(lhs, wn_ref[...], preferred_element_type=jnp.float32)

    def sigmoid(v):
        return 0.5 * jnp.tanh(0.5 * v) + 0.5

    in_top, in_bottom = my_row > 0, my_row < n_rows - 1
    in_left, in_right = my_col > 0, my_col < n_cols - 1

    def zr_chunk(s, q0, n):
        acc = conv_zr(q0, n) + gate_zr[s, q0 - 1:q0 - 1 + n].reshape(n * COMP, 256)
        z = sigmoid(acc[:, :128])
        r = sigmoid(acc[:, 128:])
        zs[q0:q0 + n] = z.reshape(n, COMP, 128)
        rh[q0:q0 + n, MARGIN - 8:MARGIN - 8 + COMP, :] = r.reshape(n, COMP, 128) * hs[q0:q0 + n, MARGIN - 8:MARGIN - 8 + COMP, :]

    def n_chunk(s, q0, n, t, last):
        g0 = (q0 - first + k - 1 - s) // 2
        acc = conv_n(q0, n) + gate_n[s, g0:g0 + n // 2].reshape(n // 2 * COMP, 256)
        both = jnp.tanh(acc).reshape(n // 2, COMP, 256)
        cand = jnp.stack([both[:, :, :128], both[:, :, 128:]], axis=1).reshape(n, COMP, 128)
        h = hs[q0:q0 + n, MARGIN - 8:MARGIN - 8 + COMP, :]
        h_new = cand + zs[q0:q0 + n] * (h - cand)
        inner = h_new[:, 8:8 + width, :]
        for i in range(n):
            q = q0 + i - first
            keep = in_top if q < 0 else in_bottom if q >= n_pairs else None
            at = pl.ds(MARGIN, width)
            hs[q0 + i, at, :] = inner[i] if keep is None else jnp.where(keep, inner[i], 0.0)
            if not last:
                for lo, inside in ((0, in_left), (8 + width, in_right)):
                    inside = inside if keep is None else jnp.logical_and(inside, keep)
                    hs[q0 + i, MARGIN - 8 + lo:MARGIN + lo, :] = jnp.where(inside, h_new[i, lo:lo + 8, :], 0.0)
            if 0 <= q < n_pairs:
                seq_ref[t, q] = inner[i].T.astype(jnp.bfloat16)

    def chunks(lo, hi, size):
        for q0 in range(lo, hi, size):
            yield q0, min(size, hi - q0)

    n_sub = x_ref.shape[1]
    edge = halo * 8
    lane2 = lax.broadcasted_iota(jnp.int32, (1, 128), 1)

    def wide(v):
        return jnp.concatenate([v, jnp.zeros((v.shape[0], 128 - v.shape[1]), v.dtype)], axis=1)

    def x_copy(d):
        di, dj = DIRS[d]
        if dj == 0:
            src = x_ref.at[:, pl.ds(0 if di < 0 else n_sub - edge, edge), :]
            dst = x_row_in.at[0 if di < 0 else 1]
        else:
            rows = {-1: pl.ds(0, edge), 1: pl.ds(n_sub - edge, edge), 0: pl.ds(0, n_sub)}[di]
            there_rows = {-1: pl.ds(edge + n_sub, edge), 1: pl.ds(0, edge), 0: pl.ds(edge, n_sub)}[di]
            side = 0 if dj < 0 else 1
            src = x_pack.at[side, rows, :]
            dst = x_col_in.at[side, there_rows, :]
        return pltpu.make_async_remote_copy(
            src_ref=src, dst_ref=dst, send_sem=x_send_sem.at[d], recv_sem=x_recv_sem.at[d],
            device_id=device(di, dj), device_id_type=pl.DeviceIdType.LOGICAL)

    def pack_x():
        for side in range(2):
            packed = jnp.zeros((n_sub, 128), jnp.float32)
            for t in range(n_steps):
                x = wide(x_ref[t].astype(jnp.float32))
                here = jnp.logical_and(lane2 >= 8 * t, lane2 < 8 * t + 8)
                packed = jnp.where(here, pltpu.roll(x, (8 * t - side * (width - 8)) % 128, 1), packed)
            x_pack[side] = packed.astype(jnp.bfloat16)

    def build_x(t, s):
        lo = lane2 < 8
        hi = lane2 >= 8 + width
        for first_sub, n, own, col in ((8, edge, x_row_in[1, t], 0), (8 + edge, n_sub, x_ref[t], edge), (8 + edge + n_sub, edge, x_row_in[0, t], edge + n_sub)):
            v = pltpu.roll(wide(own.astype(jnp.float32)), 8, 1)
            from_left = pltpu.roll(x_col_in[1, col:col + n, :].astype(jnp.float32), lax.rem(128 - 8 * t, 128), 1)
            from_right = pltpu.roll(x_col_in[0, col:col + n, :].astype(jnp.float32), lax.rem(128 + 8 + width - 8 * t, 128), 1)
            v = jnp.where(lo, from_left, jnp.where(hi, from_right, v))
            xs[0, first_sub:first_sub + n, :] = pltpu.roll(v, 1, 1)
            xs[1, first_sub:first_sub + n, :] = v
            xs[2, first_sub:first_sub + n, :] = pltpu.roll(v, 127, 1)
        zero = jnp.zeros((32, 128), jnp.bfloat16)
        for i in range(n_pairs + 2 * k):
            both = jnp.concatenate([xs[c, 16 * i:16 * i + 32].astype(jnp.bfloat16) for c in range(3)] + [zero], axis=0)
            xl[i] = both.T[:COMP]
        ext = k - 1 - s
        bias_zr = jnp.concatenate([b_ref[0:1, :], b_ref[1:2, :]], axis=1)
        bias_n = jnp.concatenate([b_ref[2:3, :], b_ref[2:3, :]], axis=1)
        for i, n in chunks(k - ext - 1, k + n_pairs + ext + 1, 2):
            part = jnp.dot(xl[i:i + n].reshape(n * COMP, 128), wxzr_ref[...], preferred_element_type=jnp.float32)
            gate_zr[s, i:i + n] = (part + bias_zr).reshape(n, COMP, 256)
        for g0, n in chunks(0, n_pairs // 2 + ext, 2):
            i = k - ext + 2 * g0
            two = xl[i:i + 2 * n].reshape(n, 2, COMP, 128)
            lhs = jnp.concatenate([two[:, 0], two[:, 1]], axis=-1).reshape(n * COMP, 256)
            part = jnp.dot(lhs, wxn_ref[...], preferred_element_type=jnp.float32)
            gate_n[s, g0:g0 + n] = (part + bias_n).reshape(n, COMP, 256)

    def fold_weights():
        def pair(get, a0, a1, gate):
            lo_part = get(a0, gate, 0) if 0 <= a0 <= 2 else None
            hi_part = get(a1, gate, 1) if 0 <= a1 <= 2 else None
            zero = jnp.zeros_like(lo_part if hi_part is None else hi_part)
            return jnp.where(lane2 < 64, zero if lo_part is None else lo_part, zero if hi_part is None else hi_part)

        for c in range(3):
            def get_h(a, gate, high):
                if gate == 2:
                    v = wide(whn_raw[a, c].astype(jnp.float32))
                    return pltpu.roll(v, 64, 1) if high else v
                v = whzr_raw[a, c].astype(jnp.float32)
                return pltpu.roll(v, 64, 1) if high != gate else v

            def get_x(a, gate, high):
                v = wx_raw[a, c].astype(jnp.float32)
                v = wide(v[:, 128:]) if gate == 2 else v[:, :128]
                return pltpu.roll(v, 64, 1) if high != (gate % 2) else v

            for j, rho in enumerate((0, 1, 2, -1)):
                at = c * 256 + j * 64
                for gate in range(2):
                    wzr_ref[at:at + 64, gate * 128:gate * 128 + 128] = pair(get_h, rho + 1, rho, gate).astype(jnp.bfloat16)
            for j, rho in enumerate((0, 1, 2, 3, 4, -1)):
                at = c * 384 + j * 64
                for o in (0, 2):
                    block = pair(get_h, rho - o + 1, rho - o, 2) if -1 <= rho - o <= 2 else jnp.zeros((64, 128), jnp.float32)
                    wn_ref[at:at + 64, o * 64:o * 64 + 128] = block.astype(jnp.bfloat16)
            for j, rho in enumerate((-1, 0, 1, 2)):
                at = c * 32 + j * 8
                for gate in range(3):
                    wx_ref[at:at + 8, gate * 128:gate * 128 + 128] = pair(get_x, rho + 1, rho, gate)
        wx_ref[96:128, :] = jnp.zeros((32, 384), jnp.float32)
        wxzr_ref[...] = wx_ref[:, :256].astype(jnp.bfloat16)
        wxn_ref[...] = jnp.zeros_like(wxn_ref)
        wxn_ref[0:128, 0:128] = wx_ref[:, 256:].astype(jnp.bfloat16)
        wxn_ref[128:256, 128:256] = wx_ref[:, 256:].astype(jnp.bfloat16)
        zr = bias_raw[:, :128]
        turned = pltpu.roll(zr, 64, 1)
        cand = wide(bias_raw[:, 128:])
        b_ref[0:1, :] = jnp.where(lane2 < 64, zr, turned)
        b_ref[1:2, :] = jnp.where(lane2 < 64, turned, zr)
        b_ref[2:3, :] = jnp.where(lane2 < 64, cand, pltpu.roll(cand, 64, 1))

    loads[0].wait()
    pack_x()
    for d, (di, dj) in enumerate(DIRS):
        @pl.when(there(di, dj))
        def _():
            x_copy(d).start()
    loads[1].wait()
    for q in range(n_pairs):
        hs[first + q, MARGIN:MARGIN + width, :] = h_ref[q].T
    send(rim, 0)
    send(middle, 0)
    for load in loads[2:]:
        load.wait()
    fold_weights()
    xs[...] = jnp.zeros_like(xs)
    for d, (di, dj) in enumerate(DIRS):
        @pl.when(there(-di, -dj))
        def _():
            x_copy(d).wait_recv()

    def zr(s, lo, hi):
        for q0, n in chunks(first + lo, first + hi, CHUNK):
            zr_chunk(s, q0, n)

    def cand(t, s, lo, hi):
        for q0, n in chunks(first + lo, first + hi, N_CHUNK):
            n_chunk(s, q0, n, t, s == k - 1)

    n_periods = n_steps // k

    def period(p, carry):
        par = lax.rem(p, 2)
        for s in range(k):
            build_x(p * k + s, s)
        for s in range(k):
            ext = k - 1 - s
            t = p * k + s
            if s == 0:
                receive(rim, par)
                zr(s, -ext - 1, RIM - 1)
                zr(s, n_pairs - RIM + 1, n_pairs + ext + 1)
                receive(middle, par)
                zr(s, RIM - 1, n_pairs - RIM + 1)
                for m, (di, dj, _) in enumerate(moves):
                    @pl.when(there(di, dj))
                    def _():
                        move(m, par).wait_send()
            if s < k - 1:
                if s > 0:
                    zr(s, -ext - 1, n_pairs + ext + 1)
                cand(t, s, -ext, n_pairs + ext)
            else:
                more = p + 1 < n_periods

                def send_next(which):
                    @pl.when(more)
                    def _():
                        send(which, 1 - par)
                if s > 0:
                    zr(s, -1, RIM + 1)
                    zr(s, n_pairs - RIM - 1, n_pairs + 1)
                cand(t, s, 0, RIM)
                cand(t, s, n_pairs - RIM, n_pairs)
                send_next(rim)
                if s > 0:
                    zr(s, RIM + 1, n_pairs - RIM - 1)
                cand(t, s, RIM, n_pairs - RIM)
                send_next(middle)
        return carry

    lax.fori_loop(0, n_steps // k, period, 0)
    for q in range(n_pairs):
        last_ref[q] = hs[first + q, MARGIN:MARGIN + width, :].T
    for d, (di, dj) in enumerate(DIRS):
        @pl.when(there(di, dj))
        def _():
            x_copy(d).wait_send()


def solution(mesh):
    n_rows = mesh.shape['rows']
    n_cols = mesh.shape['cols']
    frame_spec = P(None, 'batch', 'rows', 'cols', None)
    state_spec = P('batch', 'rows', 'cols', None)

    def local_fn(frames, h_init, w_x, w_hzr, w_hn, gate_bias):
        n_steps, _, tile_h, width, c_in = frames.shape
        n_hidden = h_init.shape[-1]
        k = FUSE
        n_pairs = tile_h // 2
        x = frames[:, 0].transpose(0, 1, 3, 2).reshape(n_steps, tile_h * c_in, width)
        h0 = h_init[0].transpose(0, 2, 1).reshape(n_pairs, 2 * n_hidden, width)
        edge = 2 * k * c_in
        n_buf = n_pairs + 2 * k + 2
        vmem = pl.BlockSpec(memory_space=pltpu.VMEM)
        seq, last = pl.pallas_call(
            functools.partial(kernel, (n_steps, n_pairs, width, n_rows, n_cols)),
            out_shape=(pltpu.VMEM((n_steps, n_pairs, 128, width), jnp.bfloat16),
                       jax.ShapeDtypeStruct((n_pairs, 128, width), jnp.float32)),
            in_specs=[pl.BlockSpec(memory_space=pltpu.HBM)] * 6,
            out_specs=(vmem, vmem),
            scratch_shapes=[
                pltpu.VMEM(x.shape, x.dtype),
                pltpu.VMEM(h0.shape, h0.dtype),
                pltpu.VMEM(w_x.shape, w_x.dtype),
                pltpu.VMEM(w_hzr.shape, w_hzr.dtype),
                pltpu.VMEM(w_hn.shape, w_hn.dtype),
                pltpu.VMEM((1, gate_bias.shape[0]), gate_bias.dtype),
                pltpu.VMEM((n_buf, 128, 128), jnp.float32),
                pltpu.VMEM((n_buf, 128, 128), jnp.float32),
                pltpu.VMEM((n_buf, COMP, 128), jnp.float32),
                pltpu.VMEM((n_pairs + 2 * k, COMP, 128), jnp.bfloat16),
                pltpu.VMEM((k, n_pairs + 2 * k, COMP, 256), jnp.float32),
                pltpu.VMEM((k, n_pairs // 2 + k - 1, COMP, 256), jnp.float32),
                pltpu.VMEM((2, 2, k, width, 128), jnp.float32),
                pltpu.VMEM((2, 2, n_pairs, 2 * k, 128), jnp.float32),
                pltpu.VMEM((2, 4, k, 2 * k, 128), jnp.float32),
                pltpu.VMEM((768, 256), jnp.bfloat16),
                pltpu.VMEM((1152, 256), jnp.bfloat16),
                pltpu.VMEM((128, 384), jnp.float32),
                pltpu.VMEM((128, 256), jnp.bfloat16),
                pltpu.VMEM((256, 256), jnp.bfloat16),
                pltpu.VMEM((3, 128), jnp.float32),
                pltpu.VMEM((3, tile_h * c_in + 2 * edge + 16, 128), jnp.float32),
                pltpu.VMEM((2, tile_h * c_in, 128), jnp.bfloat16),
                pltpu.VMEM((2, n_steps, edge, width), jnp.bfloat16),
                pltpu.VMEM((2, tile_h * c_in + 2 * edge, 128), jnp.bfloat16),
                pltpu.SemaphoreType.DMA((12,)),
                pltpu.SemaphoreType.DMA((2, 12)),
                pltpu.SemaphoreType.DMA((8,)),
                pltpu.SemaphoreType.DMA((8,)),
                pltpu.SemaphoreType.DMA((6,)),
            ],
            compiler_params=pltpu.CompilerParams(collective_id=0, has_side_effects=True, vmem_limit_bytes=32 * 2**20),
        )(*[pltpu.with_memory_space_constraint(v, pltpu.HBM) for v in (x, h0, w_x, w_hzr, w_hn, gate_bias.reshape(1, -1))])
        seq = seq.reshape(n_steps, 1, tile_h, n_hidden, width).transpose(0, 1, 2, 4, 3)
        last = last.reshape(1, tile_h, n_hidden, width).transpose(0, 1, 3, 2)
        return seq, last

    return jax.shard_map(local_fn, mesh=mesh, in_specs=(frame_spec, state_spec, P(), P(), P(), P()), out_specs=(frame_spec, state_spec), check_vma=False)
```

time: 85.3 us -> 75.5 us (0.89)
  Pallas kernels: 80.2 us -> 70.4 us
    pallas_call x1, Pallas kernels: 80.2 us -> 70.4 us  [local_fn(): pl.pallas_call(functools.partial(kernel, (n_steps, n_pairs, width, n_rows...]
where the time goes in v4:
time: 75.5 us; the launch traced here: 75.4 us
  Pallas kernels  70.4 us (93%)
  local copies, waits for them, and re-layouts  4.37 us (6%)
    pallas_call x1, Pallas kernels, local_fn(): pl.pallas_call(functools.partial(kernel, (n_steps, n_pairs, width, n_rows...  70.4 us
    unnamed x2, local copies, waits for them, and re-layouts  4.37 us

profile of v4, /device:TPU:97, one launch (start us, length us, event | category | flops | bytes accessed | tf_op | source)
XLA Modules:
  0.0 75.4 jit_solution(4834804999784032590)
XLA Ops:
  0.6 70.4 %shard_map.77 = (bf16[16,16,128,96]{3,2,1,0:T(8,128)(2,1)S(1)}, f32[16,128,96]{2,1,0:T(8,128)S(1)}) custom-call(bf16[16,256,96]{2,1,0:T(8,128)(2,1)} %bitcast.21, f32[16,128,96]{2,1,0:T(8,128)} %bitcast.22, bf16[3,3,8,192]{3,2,1,0:T(8,128)(2,1)} %wx_hbm.1, bf16[3,3,64,128]{3,2,1,0:T(8,128)(2,1)} %whzr_hbm.1, bf16[3,3,64,64]{3,2,1,0:T(8,128)(2,1)} %whn_hbm.1, ...), custom_call_target="tpu_custom_call" | custom-call | tf_op jit(solution)/shard_map/pallas_call | solution.py:361
  71.0 3.4 %copy.11 = bf16[16,1,32,96,64]{3,4,2,1,0:T(8,128)(2,1)} copy(bf16[16,1,32,96,64]{3,4,2,1,0:T(8,128)(2,1)S(1)} %bitcast.19) | data formatting | bytes 12582912
  74.4 1.0 %copy.12 = f32[1,32,96,64]{2,3,1,0:T(8,128)} copy(f32[1,32,96,64]{2,3,1,0:T(8,128)S(1)} %bitcast.20) | data formatting | bytes 1572864

commit v5 on v4

--- a/solution.py
+++ b/solution.py
@@ -7,11 +7,11 @@
 from jax.experimental.pallas import tpu as pltpu
 from jax.sharding import PartitionSpec as P
 
-FUSE = 2
+FUSE = 4
 CHUNK = 2
 N_CHUNK = 2
-RIM = 4
 MARGIN = 16
+SUBLANES = 128
 COMP = 112
 DIRS = ((-1, 0), (1, 0), (0, -1), (0, 1), (-1, -1), (-1, 1), (1, -1), (1, 1))
 
@@ -55,46 +55,43 @@
     hs[...] = jnp.zeros_like(hs)
     rh[...] = jnp.zeros_like(rh)
     n_peers = sum(there(di, dj).astype(jnp.int32) for di, dj in DIRS)
-    pl.semaphore_wait(barrier, n_peers)
-    moves = [(-1, 0, 0), (1, 0, 0)] + [(di, dj, 0) for di in (-1, 1) for dj in (-1, 1)]
-    bounds = ((0, RIM), (RIM, n_pairs - RIM), (n_pairs - RIM, n_pairs))
-    moves += [(0, dj, g) for g in range(3) for dj in (-1, 1)]
-    rim = (0, 1, 2, 3, 4, 5, 6, 7, 10, 11)
-    middle = (8, 9)
+    moves = [(-1, 0), (1, 0)] + [(di, dj) for di in (-1, 1) for dj in (-1, 1)]
+    moves += [(0, -1), (0, 1)]
+    order = (2, 3, 4, 5, 6, 7, 0, 1)
 
     def landing(m, par):
-        di, dj, g = moves[m]
+        di, dj = moves[m]
         if di == 0:
-            return col_in.at[par, (dj + 1) // 2, pl.ds(bounds[g][0], bounds[g][1] - bounds[g][0])]
+            return col_in.at[par, (dj + 1) // 2]
         return row_in.at[par, (di + 1) // 2] if dj == 0 else cor_in.at[par, m - 2]
 
     def move(m, par):
-        di, dj, g = moves[m]
+        di, dj = moves[m]
         cols = {-1: pl.ds(MARGIN, halo), 1: pl.ds(MARGIN + width - halo, halo), 0: pl.ds(MARGIN, width)}[dj]
         if di == 0:
-            rows = pl.ds(first + bounds[g][0], bounds[g][1] - bounds[g][0])
+            rows = pl.ds(first, n_pairs)
         else:
             rows = pl.ds(first if di < 0 else first + n_pairs - k, k)
         return pltpu.make_async_remote_copy(
             src_ref=hs.at[rows, cols, :], dst_ref=landing(m, par), send_sem=send_sem.at[m], recv_sem=recv_sem.at[par, m],
             device_id=device(di, dj), device_id_type=pl.DeviceIdType.LOGICAL)
 
-    def send(which, par):
-        for m in which:
+    def send(par):
+        for m in order:
             @pl.when(there(moves[m][0], moves[m][1]))
             def _():
                 move(m, par).start()
 
-    def receive(which, par):
-        for m in which:
+    def receive(par):
+        for m in order:
             @pl.when(there(-moves[m][0], -moves[m][1]))
             def _():
                 move(m, par).wait_recv()
-        for m in which:
-            di, dj, g = moves[m]
+        for m in order:
+            di, dj = moves[m]
             cols = {-1: pl.ds(MARGIN + width, halo), 1: pl.ds(MARGIN - halo, halo), 0: pl.ds(MARGIN, width)}[dj]
             if di == 0:
-                rows = pl.ds(first + bounds[g][0], bounds[g][1] - bounds[g][0])
+                rows = pl.ds(first, n_pairs)
             else:
                 rows = pl.ds(first + n_pairs if di < 0 else first - k, k)
             hs[rows, cols, :] = landing(m, par)[...]
@@ -265,6 +262,7 @@
 
     loads[0].wait()
     pack_x()
+    pl.semaphore_wait(barrier, n_peers)
     for d, (di, dj) in enumerate(DIRS):
         @pl.when(there(di, dj))
         def _():
@@ -272,8 +270,7 @@
     loads[1].wait()
     for q in range(n_pairs):
         hs[first + q, MARGIN:MARGIN + width, :] = h_ref[q].T
-    send(rim, 0)
-    send(middle, 0)
+    send(0)
     for load in loads[2:]:
         load.wait()
     fold_weights()
@@ -301,15 +298,12 @@
             ext = k - 1 - s
             t = p * k + s
             if s == 0:
-                receive(rim, par)
-                zr(s, -ext - 1, RIM - 1)
-                zr(s, n_pairs - RIM + 1, n_pairs + ext + 1)
-                receive(middle, par)
-                zr(s, RIM - 1, n_pairs - RIM + 1)
-                for m, (di, dj, _) in enumerate(moves):
+                receive(par)
+                for m, (di, dj) in enumerate(moves):
                     @pl.when(there(di, dj))
                     def _():
                         move(m, par).wait_send()
+                zr(s, -ext - 1, n_pairs + ext + 1)
             if s < k - 1:
                 if s > 0:
                     zr(s, -ext - 1, n_pairs + ext + 1)
@@ -317,20 +311,13 @@
             else:
                 more = p + 1 < n_periods
 
-                def send_next(which):
-                    @pl.when(more)
-                    def _():
-                        send(which, 1 - par)
                 if s > 0:
-                    zr(s, -1, RIM + 1)
-                    zr(s, n_pairs - RIM - 1, n_pairs + 1)
-                cand(t, s, 0, RIM)
-                cand(t, s, n_pairs - RIM, n_pairs)
-                send_next(rim)
-                if s > 0:
-                    zr(s, RIM + 1, n_pairs - RIM - 1)
-                cand(t, s, RIM, n_pairs - RIM)
-                send_next(middle)
+                    zr(s, -1, n_pairs + 1)
+                cand(t, s, 0, n_pairs)
+
+                @pl.when(more)
+                def _():
+                    send(1 - par)
         return carry
 
     lax.fori_loop(0, n_steps // k, period, 0)
@@ -371,8 +358,8 @@
                 pltpu.VMEM(w_hzr.shape, w_hzr.dtype),
                 pltpu.VMEM(w_hn.shape, w_hn.dtype),
                 pltpu.VMEM((1, gate_bias.shape[0]), gate_bias.dtype),
-                pltpu.VMEM((n_buf, 128, 128), jnp.float32),
-                pltpu.VMEM((n_buf, 128, 128), jnp.float32),
+                pltpu.VMEM((n_buf, SUBLANES, 128), jnp.float32),
+                pltpu.VMEM((n_buf, SUBLANES, 128), jnp.float32),
                 pltpu.VMEM((n_buf, COMP, 128), jnp.float32),
                 pltpu.VMEM((n_pairs + 2 * k, COMP, 128), jnp.bfloat16),
                 pltpu.VMEM((k, n_pairs + 2 * k, COMP, 256), jnp.float32),
@@ -390,13 +377,13 @@
                 pltpu.VMEM((2, tile_h * c_in, 128), jnp.bfloat16),
                 pltpu.VMEM((2, n_steps, edge, width), jnp.bfloat16),
                 pltpu.VMEM((2, tile_h * c_in + 2 * edge, 128), jnp.bfloat16),
-                pltpu.SemaphoreType.DMA((12,)),
-                pltpu.SemaphoreType.DMA((2, 12)),
+                pltpu.SemaphoreType.DMA((8,)),
+                pltpu.SemaphoreType.DMA((2, 8)),
                 pltpu.SemaphoreType.DMA((8,)),
                 pltpu.SemaphoreType.DMA((8,)),
                 pltpu.SemaphoreType.DMA((6,)),
             ],
-            compiler_params=pltpu.CompilerParams(collective_id=0, has_side_effects=True, vmem_limit_bytes=32 * 2**20),
+            compiler_params=pltpu.CompilerParams(collective_id=0, has_side_effects=True, vmem_limit_bytes=50 * 2**20),
         )(*[pltpu.with_memory_space_constraint(v, pltpu.HBM) for v in (x, h0, w_x, w_hzr, w_hn, gate_bias.reshape(1, -1))])
         seq = seq.reshape(n_steps, 1, tile_h, n_hidden, width).transpose(0, 1, 2, 4, 3)
         last = last.reshape(1, tile_h, n_hidden, width).transpose(0, 1, 3, 2)

time: 75.5 us -> 67.8 us (0.90)
  Pallas kernels: 70.4 us -> 62.7 us
    pallas_call x1, Pallas kernels: 70.4 us -> 62.7 us  [local_fn(): pl.pallas_call(functools.partial(kernel, (n_steps, n_pairs, width, n_rows...]
    unnamed x2 -> x4, local copies, waits for them, and re-layouts: 4.37 us -> 4.37 us
where the time goes in v5:
time: 67.8 us; the launch traced here: 67.7 us
  Pallas kernels  62.7 us (92%)
  local copies, waits for them, and re-layouts  4.37 us (6%)
    pallas_call x1, Pallas kernels, local_fn(): pl.pallas_call(functools.partial(kernel, (n_steps, n_pairs, width, n_rows...  62.7 us
    unnamed x4, local copies, waits for them, and re-layouts  4.37 us

profile of v5, /device:TPU:97, one launch (start us, length us, event | category | flops | bytes accessed | tf_op | source)
XLA Modules:
  0.0 67.7 jit_solution(1106458750452180733)
XLA Ops:
  0.6 62.7 %shard_map.77 = (bf16[16,16,128,96]{3,2,1,0:T(8,128)(2,1)S(1)}, f32[16,128,96]{2,1,0:T(8,128)}) custom-call(bf16[16,256,96]{2,1,0:T(8,128)(2,1)} %bitcast.20, f32[16,128,96]{2,1,0:T(8,128)} %bitcast.21, bf16[3,3,8,192]{3,2,1,0:T(8,128)(2,1)} %wx_hbm.1, bf16[3,3,64,128]{3,2,1,0:T(8,128)(2,1)} %whzr_hbm.1, bf16[3,3,64,64]{3,2,1,0:T(8,128)(2,1)} %whn_hbm.1, ...), custom_call_target="tpu_custom_call" | custom-call | tf_op jit(solution)/shard_map/pallas_call | solution.py:348
  63.3 0.0 copy-start
  63.3 3.4 %copy.11 = bf16[16,1,32,96,64]{3,4,2,1,0:T(8,128)(2,1)} copy(bf16[16,1,32,96,64]{3,4,2,1,0:T(8,128)(2,1)S(1)} %bitcast.19) | data formatting | bytes 12582912
  66.7 0.0 copy-done
  66.7 1.0 %copy.12 = f32[1,32,96,64]{2,3,1,0:T(8,128)} copy(f32[1,32,96,64]{2,3,1,0:T(8,128)S(1)} %bitcast.22) | data formatting | bytes 1572864
Async XLA Ops:
  63.3 3.4 %copy-start = (f32[16,128,96]{2,1,0:T(8,128)S(1)}, f32[16,128,96]{2,1,0:T(8,128)}, u32[]{:S(2)}) copy-start(f32[16,128,96]{2,1,0:T(8,128)} %get-tuple-element.5) | copy-start | bytes 2359300

commit v6 on v5

--- a/solution.py
+++ b/solution.py
@@ -9,7 +9,7 @@
 
 FUSE = 4
 CHUNK = 2
-N_CHUNK = 2
+N_CHUNK = 4
 MARGIN = 16
 SUBLANES = 128
 COMP = 112
@@ -163,11 +163,14 @@
     def wide(v):
         return jnp.concatenate([v, jnp.zeros((v.shape[0], 128 - v.shape[1]), v.dtype)], axis=1)
 
+    x_moves = DIRS + DIRS[:2]
+
     def x_copy(d):
-        di, dj = DIRS[d]
+        di, dj = x_moves[d]
         if dj == 0:
-            src = x_ref.at[:, pl.ds(0 if di < 0 else n_sub - edge, edge), :]
-            dst = x_row_in.at[0 if di < 0 else 1]
+            frames = pl.ds(0, k) if d < 2 else pl.ds(k, n_steps - k)
+            src = x_ref.at[frames, pl.ds(0 if di < 0 else n_sub - edge, edge), :]
+            dst = x_row_in.at[0 if di < 0 else 1, frames]
         else:
             rows = {-1: pl.ds(0, edge), 1: pl.ds(n_sub - edge, edge), 0: pl.ds(0, n_sub)}[di]
             there_rows = {-1: pl.ds(edge + n_sub, edge), 1: pl.ds(0, edge), 0: pl.ds(edge, n_sub)}[di]
@@ -263,22 +266,30 @@
     loads[0].wait()
     pack_x()
     pl.semaphore_wait(barrier, n_peers)
-    for d, (di, dj) in enumerate(DIRS):
-        @pl.when(there(di, dj))
-        def _():
-            x_copy(d).start()
+
+    def x_send(which):
+        for d in which:
+            @pl.when(there(*x_moves[d]))
+            def _():
+                x_copy(d).start()
+
+    def x_receive(which, when):
+        for d in which:
+            @pl.when(jnp.logical_and(when, there(-x_moves[d][0], -x_moves[d][1])))
+            def _():
+                x_copy(d).wait_recv()
+
+    x_send((4, 5, 6, 7, 2, 3, 0, 1))
     loads[1].wait()
     for q in range(n_pairs):
         hs[first + q, MARGIN:MARGIN + width, :] = h_ref[q].T
     send(0)
+    x_send((8, 9))
     for load in loads[2:]:
         load.wait()
     fold_weights()
     xs[...] = jnp.zeros_like(xs)
-    for d, (di, dj) in enumerate(DIRS):
-        @pl.when(there(-di, -dj))
-        def _():
-            x_copy(d).wait_recv()
+    x_receive(range(8), my_row >= 0)
 
     def zr(s, lo, hi):
         for q0, n in chunks(first + lo, first + hi, CHUNK):
@@ -299,6 +310,7 @@
             t = p * k + s
             if s == 0:
                 receive(par)
+                x_receive((8, 9), p == 0)
                 for m, (di, dj) in enumerate(moves):
                     @pl.when(there(di, dj))
                     def _():
@@ -323,7 +335,7 @@
     lax.fori_loop(0, n_steps // k, period, 0)
     for q in range(n_pairs):
         last_ref[q] = hs[first + q, MARGIN:MARGIN + width, :].T
-    for d, (di, dj) in enumerate(DIRS):
+    for d, (di, dj) in enumerate(x_moves):
         @pl.when(there(di, dj))
         def _():
             x_copy(d).wait_send()
@@ -379,8 +391,8 @@
                 pltpu.VMEM((2, tile_h * c_in + 2 * edge, 128), jnp.bfloat16),
                 pltpu.SemaphoreType.DMA((8,)),
                 pltpu.SemaphoreType.DMA((2, 8)),
-                pltpu.SemaphoreType.DMA((8,)),
-                pltpu.SemaphoreType.DMA((8,)),
+                pltpu.SemaphoreType.DMA((10,)),
+                pltpu.SemaphoreType.DMA((10,)),
                 pltpu.SemaphoreType.DMA((6,)),
             ],
             compiler_params=pltpu.CompilerParams(collective_id=0, has_side_effects=True, vmem_limit_bytes=50 * 2**20),

time: 67.8 us -> 65.7 us (0.969)
  Pallas kernels: 62.7 us -> 60.6 us
    pallas_call x1, Pallas kernels: 62.7 us -> 60.6 us  [local_fn(): pl.pallas_call(functools.partial(kernel, (n_steps, n_pairs, width, n_rows...]
where the time goes in v6:
time: 65.7 us; the launch traced here: 65.6 us
  Pallas kernels  60.6 us (92%)
  local copies, waits for them, and re-layouts  4.37 us (7%)
    pallas_call x1, Pallas kernels, local_fn(): pl.pallas_call(functools.partial(kernel, (n_steps, n_pairs, width, n_rows...  60.6 us
    unnamed x4, local copies, waits for them, and re-layouts  4.37 us

profile of v6, /device:TPU:97, one launch (start us, length us, event | category | flops | bytes accessed | tf_op | source)
XLA Modules:
  0.0 65.6 jit_solution(9540398127782116400)
XLA Ops:
  0.6 60.6 %shard_map.77 = (bf16[16,16,128,96]{3,2,1,0:T(8,128)(2,1)S(1)}, f32[16,128,96]{2,1,0:T(8,128)}) custom-call(bf16[16,256,96]{2,1,0:T(8,128)(2,1)} %bitcast.20, f32[16,128,96]{2,1,0:T(8,128)} %bitcast.21, bf16[3,3,8,192]{3,2,1,0:T(8,128)(2,1)} %wx_hbm.1, bf16[3,3,64,128]{3,2,1,0:T(8,128)(2,1)} %whzr_hbm.1, bf16[3,3,64,64]{3,2,1,0:T(8,128)(2,1)} %whn_hbm.1, ...), custom_call_target="tpu_custom_call" | custom-call | tf_op jit(solution)/shard_map/pallas_call | solution.py:360
  61.2 0.0 copy-start
  61.2 3.4 %copy.11 = bf16[16,1,32,96,64]{3,4,2,1,0:T(8,128)(2,1)} copy(bf16[16,1,32,96,64]{3,4,2,1,0:T(8,128)(2,1)S(1)} %bitcast.19) | data formatting | bytes 12582912
  64.6 0.0 copy-done
  64.6 1.0 %copy.12 = f32[1,32,96,64]{2,3,1,0:T(8,128)} copy(f32[1,32,96,64]{2,3,1,0:T(8,128)S(1)} %bitcast.22) | data formatting | bytes 1572864
Async XLA Ops:
  61.2 3.4 %copy-start = (f32[16,128,96]{2,1,0:T(8,128)S(1)}, f32[16,128,96]{2,1,0:T(8,128)}, u32[]{:S(2)}) copy-start(f32[16,128,96]{2,1,0:T(8,128)} %get-tuple-element.5) | copy-start | bytes 2359300
